TPU v7x, 512 devices: a 8x2x16 block of a 8x8x16 slice. The times are simulated.
512 devices in a mesh: snap: 2 (over y), row: 128 (over z, x), col: 2 (over core).
Axes of the slice: x: 8, y: 2, z: 16, core: 2. Of those that a mesh axis runs over, the one named last changes fastest.
The devices are a block of a 8x8x16 slice.
Arguments:
- density: bfloat16 [131072, 1024], P(('snap', 'row'), 'col'), parts along dimension 0, may hold values from -0.5 to 2
- pattern: int32 [4096, 32], P(('snap', 'row'), 'col'), parts along dimension 0, may hold values 0 or 1
- filter_mask: int32 [4096, 32], P(('snap', 'row')), parts along dimension 0, may hold values 0 or 1
Outputs:
- purified: bfloat16 [131072, 1024], P(('snap', 'row'), 'col'), parts along dimension 0
- traces: float32 [4], P('snap'), parts along dimension 0
There are 2 independent parts, one for each index of `snap`. A program takes and returns all parts, laid end to end along the dimension named above; each array names one. Nothing has to cross between parts.
All inputs are finite; a program needn't handle non-finite values. No bound on the sum of `pattern` or of `filter_mask` on one device may be relied on, other than what follows from the above.
Results may differ from a plain program's by a relative error of at most 0.006.
Values may be sent and summed in bfloat16 or wider, within the bound.
No kernel may reach another device: no remote copies, remote signals or barrier semaphores. Data moves between devices by JAX's collectives and lax.ppermute only.
A program may use at most 64 MiB of HBM per device.

v0:
```python
import functools

import jax
import jax.numpy as jnp
from jax import lax
from jax.sharding import Mesh
from jax.sharding import PartitionSpec as P

BLK = 32
ROW = ("row_0", "row_1")
ROW_COL = ("row_0", "row_1", "col")
SNAP_ROW = ("snap", "row_0", "row_1")


def laid_out(blocks, dim):
    shape = list(blocks.shape[1:])
    shape[dim] *= blocks.shape[0]
    return jnp.moveaxis(blocks, 0, dim).reshape(shape)


def copy_for_each(value, axis):
    copies = jnp.broadcast_to(value, (lax.axis_size(axis), *value.shape))
    return lax.all_to_all(copies, axis, split_axis=0, concat_axis=0, tiled=True)


def gathered_copies(value, axis, dim):
    return laid_out(copy_for_each(value, axis), dim)


def extended_2(value, sides, width):
    for axis, dim in sides:
        size, length = (lax.axis_size(axis), value.shape[dim])
        up = [(i, (i + 1) % size) for i in range(size - 1)]
        down = [(j, i) for i, j in up]
        last = lax.slice_in_dim(value, length - width, length, axis=dim)
        leading = lax.slice_in_dim(value, 0, width, axis=dim)
        before = lax.ppermute(last, axis, up)
        after = lax.ppermute(leading, axis, down)
        value = jnp.concatenate([before, value, after], axis=dim)
    return value


def over_axes(value, axes):
    return functools.reduce(lax.psum, axes, value)


def valid_slots(first_row, row_count, first_slot, slot_count, half_band, block_total):
    row_index = first_row + jnp.arange(row_count, dtype=jnp.int32)
    slot_index = first_slot + jnp.arange(slot_count, dtype=jnp.int32)
    column_index = row_index[:, None] + slot_index[None, :] - half_band
    return ((column_index >= 0) & (column_index < block_total)).astype(jnp.int32)


def expand_mask(values, keep_mask):
    block_rows = keep_mask.shape[0]
    slot_count = keep_mask.shape[1]
    blocks = values.reshape(block_rows, BLK, slot_count, BLK)
    blocks = blocks * keep_mask.astype(values.dtype)[:, None, :, None]
    return blocks.reshape(block_rows * BLK, slot_count * BLK)


def shift_slots(segment, moved):
    height = segment.shape[0]
    if moved > 0:
        return jnp.concatenate(
            [
                jnp.zeros((height, moved * BLK), segment.dtype),
                segment[:, : segment.shape[1] - moved * BLK],
            ],
            1,
        )
    if moved < 0:
        return jnp.concatenate(
            [segment[:, -moved * BLK :], jnp.zeros((height, -moved * BLK), segment.dtype)], 1
        )
    return segment


def band_part(left, extended, first_slot, column_slots, slot_count, half_band):
    block_rows = left.shape[0] // BLK
    byte_limit = 4 * 1024 * 1024
    group_rows = 1
    for candidate in (8, 4, 2):
        if (
            block_rows % candidate == 0
            and candidate * slot_count * BLK * column_slots * BLK * 2 <= byte_limit
        ):
            group_rows = candidate
            break

    def one_group(group):
        first = group * group_rows
        stacked = []
        for offset in range(slot_count):
            segment = lax.dynamic_slice_in_dim(
                extended, (first + offset) * BLK, group_rows * BLK, 0
            )
            segment = shift_slots(segment, offset - half_band)
            segment = lax.dynamic_slice_in_dim(segment, first_slot * BLK, column_slots * BLK, 1)
            stacked.append(segment.reshape(group_rows, BLK, column_slots * BLK))
        gathered = jnp.stack(stacked, 1).reshape(group_rows, slot_count * BLK, column_slots * BLK)
        left_rows = lax.dynamic_slice_in_dim(left, first * BLK, group_rows * BLK, 0).reshape(
            group_rows, BLK, slot_count * BLK
        )
        result = jnp.einsum("gak,gkn->gan", left_rows, gathered, preferred_element_type=jnp.float32)
        return result.reshape(group_rows * BLK, column_slots * BLK)

    result = lax.map(one_group, jnp.arange(block_rows // group_rows, dtype=jnp.int32))
    return result.reshape(block_rows * BLK, column_slots * BLK)


def diagonal_sum(values, chosen):
    block_rows = values.shape[0] // BLK
    slot_total = values.shape[1] // BLK
    diagonal = jnp.diagonal(values.reshape(block_rows, BLK, slot_total, BLK), axis1=1, axis2=3)
    return jnp.sum(diagonal.astype(jnp.float32) * chosen[None, :, None])


def slot_products(
    full_rows, extended, own_filter, first_slot, half_slots, slot_count, half_band, collect
):
    square = band_part(full_rows, extended, first_slot, half_slots, slot_count, half_band)
    squared = expand_mask(square, own_filter).astype(jnp.bfloat16)
    squared_rows = collect(squared)
    cube = band_part(squared_rows, extended, first_slot, half_slots, slot_count, half_band)
    purified = (3.0 * squared.astype(jnp.float32) - 2.0 * expand_mask(cube, own_filter)).astype(
        jnp.bfloat16
    )
    return (purified, squared)


def per_device(density, pattern, filter_mask):
    half_slots = density.shape[1] // BLK
    slot_count = 2 * half_slots
    block_rows = density.shape[0] // BLK
    col_id = lax.axis_index("col")
    row_id = lax.axis_index(ROW)
    block_total = block_rows * lax.axis_size(ROW)
    first_slot = col_id * half_slots
    own_valid = valid_slots(
        row_id * block_rows, block_rows, first_slot, half_slots, half_slots, block_total
    )
    kept = expand_mask(density, pattern * own_valid)
    chosen = (first_slot + jnp.arange(half_slots, dtype=jnp.int32) == half_slots).astype(
        jnp.float32
    )
    trace_kept = diagonal_sum(kept, chosen)
    own_filter = lax.dynamic_slice_in_dim(filter_mask, first_slot, half_slots, 1) * own_valid
    full_rows = gathered_copies(kept, "col", 1)
    extended = extended_2(full_rows, ((ROW, 0),), half_slots * BLK)

    def collect_whole(squared):
        return lax.all_gather(squared, "col", axis=1, tiled=True)

    purified, squared = slot_products(
        full_rows,
        extended,
        own_filter,
        first_slot,
        half_slots,
        slot_count,
        half_slots,
        collect_whole,
    )
    trace_squared = diagonal_sum(squared, chosen)
    total_kept, total_squared = (over_axes(trace_kept, ROW_COL), over_axes(trace_squared, ROW_COL))
    order_total = block_total * BLK
    traces = jnp.stack([total_kept, total_squared]) / order_total
    return (purified, traces)


def solution(mesh):
    finer = Mesh(
        mesh.devices.reshape(mesh.shape["snap"], 16, 8, mesh.shape["col"]),
        ("snap", "row_0", "row_1", "col"),
    )
    placed = (P(SNAP_ROW, "col"), P(SNAP_ROW, "col"), P(SNAP_ROW, None))
    return jax.shard_map(
        per_device,
        mesh=finer,
        in_specs=placed,
        out_specs=(P(SNAP_ROW, "col"), P("snap")),
        check_vma=False,
    )
```

profile of v0, /device:TPU:65, one launch (start us, length us, event | category | flops | bytes accessed | tf_op | source)
XLA Modules:
  0.0 567.0 jit_solution(4762109875554690151)
XLA Ops:
  8.5 2.1 mul.808
  10.8 45.6 %all_to_all.5 = bf16[2,512,512]{2,1,0:T(8,128)(2,1)S(1)} all-to-all(bf16[2,512,512]{2,1,0:T(8,128)(2,1)S(1)} %broadcast_in_dim.31), channel_id=1, replica_groups=mesh['snap'=2,'row_0'=16,'row_1'=8,'col'=2] {'col'}, dimensions={0} | all-to-all | bytes 2097152 | tf_op jit(solution)/shard_map/all_to_all | solution.py:23
  57.0 2.4 collective-permute-start
  60.8 2.7 reshape.773
  63.6 4.3 copy.19
  67.9 2.4 mul.812.clone
  70.3 4.4 mul.813
  74.7 6.0 %collective-permute-done = bf16[512,1024]{0,1:T(8,128)(2,1)} collective-permute-done((bf16[512,1024]{0,1:T(8,128)(2,1)S(1)}, bf16[512,1024]{0,1:T(8,128)(2,1)}, u32[]{:S(2)}, u32[]{:S(2)}) %collective-permute-start) | collective-permute-done | bytes 1048608 | tf_op jit(solution)/shard_map/ppermute | solution.py:37
  80.7 5.0 collective-permute-done.1
  85.7 3.0 pad_maximum_fusion
  88.7 3.2 copy.16
  93.1 190.5 %while.26 = (s32[]{:T(128)}, f32[4,128,512]{2,1,0:T(8,128)}, s32[4]{0:T(128)S(1)}, bf16[512,1024]{0,1:T(8,128)(2,1)}, bf16[1536,1024]{1,0:T(8,128)(2,1)S(1)}, /*...) while((s32[]{:T(128)}, f32[4,128,512]{2,1,0:T(8,128)}, ...), condition=%wide.region_1.2_spmd, body=%wide.region_0.1_spmd.sunk | while | flops 134217904 | bytes 44142148 | solution.py:108
  99.8 1.6 constant_dynamic-update-slice_fusion.130
  134.2 1.7 constant_dynamic-slice_fusion.64
  136.9 3.0 fusion.27
  147.4 1.6 constant_dynamic-update-slice_fusion.130
  181.8 1.7 constant_dynamic-slice_fusion.64
  184.5 3.0 fusion.27
  195.0 1.6 constant_dynamic-update-slice_fusion.130
  229.4 1.7 constant_dynamic-slice_fusion.64
  232.1 3.0 fusion.27
  277.0 1.7 constant_dynamic-slice_fusion.64
  279.8 3.0 fusion.27
  283.5 2.5 fusion.4
  286.1 4.5 multiply_bitcast_fusion
  290.5 2.8 gather_fusion
  293.4 3.9 reshape_reshape.10
  297.3 7.2 %copy.20 = f32[16,32,16,32]{2,0,3,1:T(8,128)} copy(f32[16,32,16,32]{3,2,1,0:T(8,128)} %reshape_reshape.10) | data formatting | bytes 2097152 | tf_op jit(solution)/shard_map/reshape;reshape | solution.py:57
  304.5 6.6 %fusion = bf16[16,16,32,32]{1,0,3,2:T(8,128)(2,1)} fusion(f32[16,32,16,32]{2,0,3,1:T(8,128)} %copy.20, f32[16,16]{1,0:T(8,128)S(1)} %get-tuple-element.421), kind=kLoop, calls=%fused_computation.163 | loop fusion | flops 524288 | bytes 1573888 | tf_op jit(solution)/shard_map/jit(diagonal)/transpose | solution.py:115
  311.1 2.8 gather_fusion.1
  314.7 23.2 %all-reduce.62 = (f32[]{:T(128)}, f32[]{:T(128)}) all-reduce(f32[]{:T(128)} %get-tuple-element.261, f32[]{:T(128)} %get-tuple-element.260), channel_id=1, replica_groups=mesh['snap'=2,'row_0'=16,'row_1'=8,'col'=2] {'row_0'}, use_global_device_ids=true, to_apply=%region_9.10 | all-reduce | flops 2 | bytes 16 | tf_op jit(solution)/shard_map/psum | solution.py:44
  337.9 15.3 %all-reduce.63 = (f32[]{:T(128)}, f32[]{:T(128)}) all-reduce(f32[]{:T(128)} %get-tuple-element.290, f32[]{:T(128)} %get-tuple-element.291), channel_id=1, replica_groups=mesh['snap'=2,'row_0'=16,'row_1'=8,'col'=2] {'row_1'}, use_global_device_ids=true, to_apply=%region_10.11 | all-reduce | flops 2 | bytes 16 | tf_op jit(solution)/shard_map/psum | solution.py:44
  353.3 15.0 %all-reduce.64 = (f32[1]{0:T(128)}, f32[1]{0:T(128)}) all-reduce(f32[1]{0:T(128)} %bitcast.143, f32[1]{0:T(128)} %bitcast.141), channel_id=1, replica_groups=mesh['snap'=2,'row_0'=16,'row_1'=8,'col'=2] {'col'}, use_global_device_ids=true, to_apply=%region_11.12 | all-reduce | flops 2 | bytes 16 | tf_op jit(solution)/shard_map/psum | solution.py:44
  368.3 1.8 maximum_multiply_fusion
  371.2 186.2 %while.27 = (s32[]{:T(128)}, f32[4,128,512]{2,1,0:T(8,128)}, s32[4]{0:T(128)S(1)}, bf16[512,1024]{1,0:T(8,128)(2,1)}, bf16[1536,1024]{1,0:T(8,128)(2,1)S(1)}, /*...) while((s32[]{:T(128)}, f32[4,128,512]{2,1,0:T(8,128)}, ...), condition=%wide.region_3.4_spmd, body=%wide.region_2.3_spmd.sunk | while | flops 134217904 | bytes 43617860 | solution.py:108
  376.4 1.6 constant_dynamic-update-slice_fusion.161
  378.0 1.6 constant_dynamic-update-slice_fusion.162
  414.0 3.0 fusion.31
  422.9 1.6 constant_dynamic-update-slice_fusion.161
  424.5 1.6 constant_dynamic-update-slice_fusion.162
  460.6 3.0 fusion.31
  469.5 1.6 constant_dynamic-update-slice_fusion.161
  471.0 1.6 constant_dynamic-update-slice_fusion.162
  507.1 3.0 fusion.31
  516.0 1.6 constant_dynamic-update-slice_fusion.161
  517.6 1.6 constant_dynamic-update-slice_fusion.162
  553.7 3.0 fusion.31
  557.4 2.8 fusion.3
  (706 shorter events, 322.7 us)
Async XLA Ops:
  7.2 362.9 %all-gather.2.cloned.1.call-start = ((), (), s32[]{:S(2)}) async-start(), calls=%async_computation.1 | async-start | bytes 1572864 | tf_op jit(solution)/shard_map/all_gather | solution.py:153
  57.0 28.8 %copy-start.20 = (bf16[2,512,512]{1,2,0:T(8,128)(2,1)}, bf16[2,512,512]{1,2,0:T(8,128)(2,1)S(1)}, u32[]{:S(2)}) copy-start(bf16[2,512,512]{1,2,0:T(8,128)(2,1)S(1)} %copy.14) | copy-start | bytes 3145732
  57.0 23.7 %collective-permute-start = (bf16[512,1024]{0,1:T(8,128)(2,1)S(1)}, bf16[512,1024]{0,1:T(8,128)(2,1)}, u32[]{:S(2)}, u32[]{:S(2)}) collective-permute-start(bf16[512,1024]{0,1:T(8,128)(2,1)S(1)} %bitcast.513), channel_id=1, source_target_pairs={{0,2},{2,4},{4,6},{6,8},{8,10},{10,12},{12,14},{14,16},{16,18},{18... | collective-permute-start | bytes 3145736 | tf_op jit(solution)/shard_map/ppermute | solution.py:37
  59.3 26.4 %collective-permute-start.1 = (bf16[512,1024]{0,1:T(8,128)(2,1)S(1)}, bf16[512,1024]{0,1:T(8,128)(2,1)}, u32[]{:S(2)}, u32[]{:S(2)}) collective-permute-start(bf16[512,1024]{0,1:T(8,128)(2,1)S(1)} %bitcast.514), channel_id=1, source_target_pairs={{2,0},{4,2},{6,4},{8,6},{10,8},{12,10},{14,12},{16,14},{18,16},{20... | collective-permute-start | bytes 3145736 | tf_op jit(solution)/shard_map/ppermute | solution.py:38
  119.7 10.1 %copy-start.4 = (bf16[128,704]{1,0:T(8,128)(2,1)S(1)}, bf16[128,704]{1,0:T(8,128)(2,1)}, u32[]{:S(2)}) copy-start(bf16[128,704]{1,0:T(8,128)(2,1)} %get-tuple-element.678) | copy-start | bytes 540676 | tf_op jit(solution)/shard_map/while
  119.7 11.6 %copy-start.16 = (bf16[128,640]{1,0:T(8,128)(2,1)S(1)}, bf16[128,640]{1,0:T(8,128)(2,1)}, u32[]{:S(2)}) copy-start(bf16[128,640]{1,0:T(8,128)(2,1)} %get-tuple-element.682) | copy-start | bytes 491524 | tf_op jit(solution)/shard_map/while
  119.7 11.6 %copy-start.18 = (bf16[128,608]{1,0:T(8,128)(2,1)S(1)}, bf16[128,608]{1,0:T(8,128)(2,1)}, u32[]{:S(2)}) copy-start(bf16[128,608]{1,0:T(8,128)(2,1)} %get-tuple-element.681) | copy-start | bytes 466948 | tf_op jit(solution)/shard_map/while
  120.0 12.7 %copy-start.12 = (bf16[128,576]{1,0:T(8,128)(2,1)S(1)}, bf16[128,576]{1,0:T(8,128)(2,1)}, u32[]{:S(2)}) copy-start(bf16[128,576]{1,0:T(8,128)(2,1)} %get-tuple-element.686) | copy-start | bytes 442372 | tf_op jit(solution)/shard_map/while
  120.0 12.7 %copy-start.14 = (bf16[128,544]{1,0:T(8,128)(2,1)S(1)}, bf16[128,544]{1,0:T(8,128)(2,1)}, u32[]{:S(2)}) copy-start(bf16[128,544]{1,0:T(8,128)(2,1)} %get-tuple-element.685) | copy-start | bytes 417796 | tf_op jit(solution)/shard_map/while
  167.2 10.1 %copy-start.4 = (bf16[128,704]{1,0:T(8,128)(2,1)S(1)}, bf16[128,704]{1,0:T(8,128)(2,1)}, u32[]{:S(2)}) copy-start(bf16[128,704]{1,0:T(8,128)(2,1)} %get-tuple-element.678) | copy-start | bytes 540676 | tf_op jit(solution)/shard_map/while
  167.3 11.6 %copy-start.16 = (bf16[128,640]{1,0:T(8,128)(2,1)S(1)}, bf16[128,640]{1,0:T(8,128)(2,1)}, u32[]{:S(2)}) copy-start(bf16[128,640]{1,0:T(8,128)(2,1)} %get-tuple-element.682) | copy-start | bytes 491524 | tf_op jit(solution)/shard_map/while
  167.3 11.6 %copy-start.18 = (bf16[128,608]{1,0:T(8,128)(2,1)S(1)}, bf16[128,608]{1,0:T(8,128)(2,1)}, u32[]{:S(2)}) copy-start(bf16[128,608]{1,0:T(8,128)(2,1)} %get-tuple-element.681) | copy-start | bytes 466948 | tf_op jit(solution)/shard_map/while
  167.6 12.7 %copy-start.12 = (bf16[128,576]{1,0:T(8,128)(2,1)S(1)}, bf16[128,576]{1,0:T(8,128)(2,1)}, u32[]{:S(2)}) copy-start(bf16[128,576]{1,0:T(8,128)(2,1)} %get-tuple-element.686) | copy-start | bytes 442372 | tf_op jit(solution)/shard_map/while
  167.6 12.7 %copy-start.14 = (bf16[128,544]{1,0:T(8,128)(2,1)S(1)}, bf16[128,544]{1,0:T(8,128)(2,1)}, u32[]{:S(2)}) copy-start(bf16[128,544]{1,0:T(8,128)(2,1)} %get-tuple-element.685) | copy-start | bytes 417796 | tf_op jit(solution)/shard_map/while
  214.8 10.1 %copy-start.4 = (bf16[128,704]{1,0:T(8,128)(2,1)S(1)}, bf16[128,704]{1,0:T(8,128)(2,1)}, u32[]{:S(2)}) copy-start(bf16[128,704]{1,0:T(8,128)(2,1)} %get-tuple-element.678) | copy-start | bytes 540676 | tf_op jit(solution)/shard_map/while
  214.9 11.6 %copy-start.16 = (bf16[128,640]{1,0:T(8,128)(2,1)S(1)}, bf16[128,640]{1,0:T(8,128)(2,1)}, u32[]{:S(2)}) copy-start(bf16[128,640]{1,0:T(8,128)(2,1)} %get-tuple-element.682) | copy-start | bytes 491524 | tf_op jit(solution)/shard_map/while
  214.9 11.6 %copy-start.18 = (bf16[128,608]{1,0:T(8,128)(2,1)S(1)}, bf16[128,608]{1,0:T(8,128)(2,1)}, u32[]{:S(2)}) copy-start(bf16[128,608]{1,0:T(8,128)(2,1)} %get-tuple-element.681) | copy-start | bytes 466948 | tf_op jit(solution)/shard_map/while
  215.2 12.7 %copy-start.12 = (bf16[128,576]{1,0:T(8,128)(2,1)S(1)}, bf16[128,576]{1,0:T(8,128)(2,1)}, u32[]{:S(2)}) copy-start(bf16[128,576]{1,0:T(8,128)(2,1)} %get-tuple-element.686) | copy-start | bytes 442372 | tf_op jit(solution)/shard_map/while
  215.2 12.7 %copy-start.14 = (bf16[128,544]{1,0:T(8,128)(2,1)S(1)}, bf16[128,544]{1,0:T(8,128)(2,1)}, u32[]{:S(2)}) copy-start(bf16[128,544]{1,0:T(8,128)(2,1)} %get-tuple-element.685) | copy-start | bytes 417796 | tf_op jit(solution)/shard_map/while
  262.5 10.1 %copy-start.4 = (bf16[128,704]{1,0:T(8,128)(2,1)S(1)}, bf16[128,704]{1,0:T(8,128)(2,1)}, u32[]{:S(2)}) copy-start(bf16[128,704]{1,0:T(8,128)(2,1)} %get-tuple-element.678) | copy-start | bytes 540676 | tf_op jit(solution)/shard_map/while
  262.5 11.6 %copy-start.16 = (bf16[128,640]{1,0:T(8,128)(2,1)S(1)}, bf16[128,640]{1,0:T(8,128)(2,1)}, u32[]{:S(2)}) copy-start(bf16[128,640]{1,0:T(8,128)(2,1)} %get-tuple-element.682) | copy-start | bytes 491524 | tf_op jit(solution)/shard_map/while
  262.5 11.6 %copy-start.18 = (bf16[128,608]{1,0:T(8,128)(2,1)S(1)}, bf16[128,608]{1,0:T(8,128)(2,1)}, u32[]{:S(2)}) copy-start(bf16[128,608]{1,0:T(8,128)(2,1)} %get-tuple-element.681) | copy-start | bytes 466948 | tf_op jit(solution)/shard_map/while
  262.8 12.7 %copy-start.12 = (bf16[128,576]{1,0:T(8,128)(2,1)S(1)}, bf16[128,576]{1,0:T(8,128)(2,1)}, u32[]{:S(2)}) copy-start(bf16[128,576]{1,0:T(8,128)(2,1)} %get-tuple-element.686) | copy-start | bytes 442372 | tf_op jit(solution)/shard_map/while
  262.8 12.7 %copy-start.14 = (bf16[128,544]{1,0:T(8,128)(2,1)S(1)}, bf16[128,544]{1,0:T(8,128)(2,1)}, u32[]{:S(2)}) copy-start(bf16[128,544]{1,0:T(8,128)(2,1)} %get-tuple-element.685) | copy-start | bytes 417796 | tf_op jit(solution)/shard_map/while
  398.3 10.3 %copy-start.5 = (bf16[128,704]{1,0:T(8,128)(2,1)S(1)}, bf16[128,704]{1,0:T(8,128)(2,1)}, u32[]{:S(2)}) copy-start(bf16[128,704]{1,0:T(8,128)(2,1)} %get-tuple-element.747) | copy-start | bytes 540676 | tf_op jit(solution)/shard_map/while
  398.3 10.3 %copy-start.7 = (bf16[128,672]{1,0:T(8,128)(2,1)S(1)}, bf16[128,672]{1,0:T(8,128)(2,1)}, u32[]{:S(2)}) copy-start(bf16[128,672]{1,0:T(8,128)(2,1)} %get-tuple-element.746) | copy-start | bytes 516100 | tf_op jit(solution)/shard_map/while
  398.3 11.8 %copy-start.17 = (bf16[128,640]{1,0:T(8,128)(2,1)S(1)}, bf16[128,640]{1,0:T(8,128)(2,1)}, u32[]{:S(2)}) copy-start(bf16[128,640]{1,0:T(8,128)(2,1)} %get-tuple-element.751) | copy-start | bytes 491524 | tf_op jit(solution)/shard_map/while
  398.3 11.8 %copy-start.19 = (bf16[128,608]{1,0:T(8,128)(2,1)S(1)}, bf16[128,608]{1,0:T(8,128)(2,1)}, u32[]{:S(2)}) copy-start(bf16[128,608]{1,0:T(8,128)(2,1)} %get-tuple-element.750) | copy-start | bytes 466948 | tf_op jit(solution)/shard_map/while
  398.6 12.9 %copy-start.13 = (bf16[128,576]{1,0:T(8,128)(2,1)S(1)}, bf16[128,576]{1,0:T(8,128)(2,1)}, u32[]{:S(2)}) copy-start(bf16[128,576]{1,0:T(8,128)(2,1)} %get-tuple-element.755) | copy-start | bytes 442372 | tf_op jit(solution)/shard_map/while
  398.6 12.9 %copy-start.15 = (bf16[128,544]{1,0:T(8,128)(2,1)S(1)}, bf16[128,544]{1,0:T(8,128)(2,1)}, u32[]{:S(2)}) copy-start(bf16[128,544]{1,0:T(8,128)(2,1)} %get-tuple-element.754) | copy-start | bytes 417796 | tf_op jit(solution)/shard_map/while
  444.8 10.3 %copy-start.5 = (bf16[128,704]{1,0:T(8,128)(2,1)S(1)}, bf16[128,704]{1,0:T(8,128)(2,1)}, u32[]{:S(2)}) copy-start(bf16[128,704]{1,0:T(8,128)(2,1)} %get-tuple-element.747) | copy-start | bytes 540676 | tf_op jit(solution)/shard_map/while
  444.8 10.3 %copy-start.7 = (bf16[128,672]{1,0:T(8,128)(2,1)S(1)}, bf16[128,672]{1,0:T(8,128)(2,1)}, u32[]{:S(2)}) copy-start(bf16[128,672]{1,0:T(8,128)(2,1)} %get-tuple-element.746) | copy-start | bytes 516100 | tf_op jit(solution)/shard_map/while
  444.8 11.8 %copy-start.17 = (bf16[128,640]{1,0:T(8,128)(2,1)S(1)}, bf16[128,640]{1,0:T(8,128)(2,1)}, u32[]{:S(2)}) copy-start(bf16[128,640]{1,0:T(8,128)(2,1)} %get-tuple-element.751) | copy-start | bytes 491524 | tf_op jit(solution)/shard_map/while
  444.8 11.8 %copy-start.19 = (bf16[128,608]{1,0:T(8,128)(2,1)S(1)}, bf16[128,608]{1,0:T(8,128)(2,1)}, u32[]{:S(2)}) copy-start(bf16[128,608]{1,0:T(8,128)(2,1)} %get-tuple-element.750) | copy-start | bytes 466948 | tf_op jit(solution)/shard_map/while
  445.1 12.9 %copy-start.13 = (bf16[128,576]{1,0:T(8,128)(2,1)S(1)}, bf16[128,576]{1,0:T(8,128)(2,1)}, u32[]{:S(2)}) copy-start(bf16[128,576]{1,0:T(8,128)(2,1)} %get-tuple-element.755) | copy-start | bytes 442372 | tf_op jit(solution)/shard_map/while
  445.1 12.9 %copy-start.15 = (bf16[128,544]{1,0:T(8,128)(2,1)S(1)}, bf16[128,544]{1,0:T(8,128)(2,1)}, u32[]{:S(2)}) copy-start(bf16[128,544]{1,0:T(8,128)(2,1)} %get-tuple-element.754) | copy-start | bytes 417796 | tf_op jit(solution)/shard_map/while
  491.3 10.3 %copy-start.5 = (bf16[128,704]{1,0:T(8,128)(2,1)S(1)}, bf16[128,704]{1,0:T(8,128)(2,1)}, u32[]{:S(2)}) copy-start(bf16[128,704]{1,0:T(8,128)(2,1)} %get-tuple-element.747) | copy-start | bytes 540676 | tf_op jit(solution)/shard_map/while
  491.4 10.3 %copy-start.7 = (bf16[128,672]{1,0:T(8,128)(2,1)S(1)}, bf16[128,672]{1,0:T(8,128)(2,1)}, u32[]{:S(2)}) copy-start(bf16[128,672]{1,0:T(8,128)(2,1)} %get-tuple-element.746) | copy-start | bytes 516100 | tf_op jit(solution)/shard_map/while
  491.4 11.8 %copy-start.17 = (bf16[128,640]{1,0:T(8,128)(2,1)S(1)}, bf16[128,640]{1,0:T(8,128)(2,1)}, u32[]{:S(2)}) copy-start(bf16[128,640]{1,0:T(8,128)(2,1)} %get-tuple-element.751) | copy-start | bytes 491524 | tf_op jit(solution)/shard_map/while
  491.4 11.8 %copy-start.19 = (bf16[128,608]{1,0:T(8,128)(2,1)S(1)}, bf16[128,608]{1,0:T(8,128)(2,1)}, u32[]{:S(2)}) copy-start(bf16[128,608]{1,0:T(8,128)(2,1)} %get-tuple-element.750) | copy-start | bytes 466948 | tf_op jit(solution)/shard_map/while
  491.7 12.9 %copy-start.13 = (bf16[128,576]{1,0:T(8,128)(2,1)S(1)}, bf16[128,576]{1,0:T(8,128)(2,1)}, u32[]{:S(2)}) copy-start(bf16[128,576]{1,0:T(8,128)(2,1)} %get-tuple-element.755) | copy-start | bytes 442372 | tf_op jit(solution)/shard_map/while
  491.7 12.9 %copy-start.15 = (bf16[128,544]{1,0:T(8,128)(2,1)S(1)}, bf16[128,544]{1,0:T(8,128)(2,1)}, u32[]{:S(2)}) copy-start(bf16[128,544]{1,0:T(8,128)(2,1)} %get-tuple-element.754) | copy-start | bytes 417796 | tf_op jit(solution)/shard_map/while
  537.9 10.3 %copy-start.5 = (bf16[128,704]{1,0:T(8,128)(2,1)S(1)}, bf16[128,704]{1,0:T(8,128)(2,1)}, u32[]{:S(2)}) copy-start(bf16[128,704]{1,0:T(8,128)(2,1)} %get-tuple-element.747) | copy-start | bytes 540676 | tf_op jit(solution)/shard_map/while
  537.9 10.3 %copy-start.7 = (bf16[128,672]{1,0:T(8,128)(2,1)S(1)}, bf16[128,672]{1,0:T(8,128)(2,1)}, u32[]{:S(2)}) copy-start(bf16[128,672]{1,0:T(8,128)(2,1)} %get-tuple-element.746) | copy-start | bytes 516100 | tf_op jit(solution)/shard_map/while
  537.9 11.8 %copy-start.17 = (bf16[128,640]{1,0:T(8,128)(2,1)S(1)}, bf16[128,640]{1,0:T(8,128)(2,1)}, u32[]{:S(2)}) copy-start(bf16[128,640]{1,0:T(8,128)(2,1)} %get-tuple-element.751) | copy-start | bytes 491524 | tf_op jit(solution)/shard_map/while
  537.9 11.8 %copy-start.19 = (bf16[128,608]{1,0:T(8,128)(2,1)S(1)}, bf16[128,608]{1,0:T(8,128)(2,1)}, u32[]{:S(2)}) copy-start(bf16[128,608]{1,0:T(8,128)(2,1)} %get-tuple-element.750) | copy-start | bytes 466948 | tf_op jit(solution)/shard_map/while
  538.2 12.9 %copy-start.13 = (bf16[128,576]{1,0:T(8,128)(2,1)S(1)}, bf16[128,576]{1,0:T(8,128)(2,1)}, u32[]{:S(2)}) copy-start(bf16[128,576]{1,0:T(8,128)(2,1)} %get-tuple-element.755) | copy-start | bytes 442372 | tf_op jit(solution)/shard_map/while
  538.2 12.9 %copy-start.15 = (bf16[128,544]{1,0:T(8,128)(2,1)S(1)}, bf16[128,544]{1,0:T(8,128)(2,1)}, u32[]{:S(2)}) copy-start(bf16[128,544]{1,0:T(8,128)(2,1)} %get-tuple-element.754) | copy-start | bytes 417796 | tf_op jit(solution)/shard_map/while
  (37 other events, 298.9 us)
Sparse Core Ops, SparseCore 0:
  286.2 18.8 all-gather.1
where the time goes:
time: 569 us; the launch traced here: 567 us
  local copies, waits for them, and re-layouts  379 us (67%)
  blocking collectives  99.3 us (17%)
  matrix products  23.9 us (4%)
  other arithmetic  22.8 us (4%)
  between operations  14.2 us (2%)
  loops' own time  12.5 us (2%)
  waiting for transfers between devices  11.1 us (2%)
    while x408, local copies, waits for them, and re-layouts  180 us
    slice x120, local copies, waits for them, and re-layouts, shift_slots(): segment[:, :segment.shape[1] - moved * BLK]  87 us
    psum x3, blocking collectives, over_axes(): return functools.reduce(lax.psum, axes, value)  53.6 us
    all_to_all x1, blocking collectives, copy_for_each(): return lax.all_to_all(copies, axis, split_axis=0, concat_axis=0, tiled=True)  45.6 us
    dynamic_slice x136, local copies, waits for them, and re-layouts, one_group(): lax.dynamic_slice_in_dim(segment, first_slot * BLK, column_slots * BLK, 1)  41.9 us
    dot_general x8, matrix products, one_group(): jnp.einsum('gak,gkn->gan', left_rows, gathered, preferred_element_type=jn...  23.9 us
    dynamic_slice x12, local copies, waits for them, and re-layouts, one_group(): lax.dynamic_slice_in_dim(left, first * BLK, group_rows * BLK, 0)  14.9 us
    another operation x2, loops' own time, band_part(): lax.map(one_group, jnp.arange(block_rows // group_rows, dtype=jnp.int32))  12.5 us
  transfers between devices with their start and end apart: 3, of which 2 were waited for; matrix products, arithmetic and copies ran while one was open for 8% of the time, Pallas kernels for 0%

commit v1 on v0

v1 whole, which is shorter than its diff:
```python
import functools

import jax
import jax.numpy as jnp
from jax import lax
from jax.experimental import pallas as pl
from jax.experimental.pallas import tpu as pltpu
from jax.sharding import PartitionSpec as P

BLK = 32
LANES = 128
TILE = 256
SNAP_ROW = ("snap", "row")


def spread(mask, width):
    slots = mask.shape[1]
    slot = lax.broadcasted_iota(jnp.int32, (slots, width), 0)
    lane = lax.broadcasted_iota(jnp.int32, (slots, width), 1)
    chosen = (lane // BLK == slot).astype(jnp.bfloat16)
    return jnp.dot(
        mask.astype(jnp.bfloat16), chosen, preferred_element_type=jnp.float32
    )


def placed(rows, start, width):
    height, length = rows.shape
    if start < 0:
        rows = rows[:, -start:]
        length += start
        start = 0
    if start + length > width:
        length = width - start
        rows = rows[:, :length]
    parts = []
    if start:
        parts.append(jnp.zeros((height, start), rows.dtype))
    parts.append(rows)
    if start + length < width:
        parts.append(jnp.zeros((height, width - start - length), rows.dtype))
    return jnp.concatenate(parts, 1) if len(parts) > 1 else rows


def eye_sum(ref, lane_start):
    row = lax.broadcasted_iota(jnp.int32, (LANES, LANES), 0)
    lane = lax.broadcasted_iota(jnp.int32, (LANES, LANES), 1)
    total = jnp.zeros((1, LANES), jnp.float32)
    for k in range(ref.shape[0] // LANES):
        part = ref[pl.ds(k * LANES, LANES), pl.ds(lane_start + k * LANES, LANES)]
        part = jnp.where(row == lane, part.astype(jnp.float32), 0.0)
        total += jnp.sum(part, axis=0, keepdims=True)
    return total


def purify_kernel(
    col_ref, filter_ref, own_a, own_b, up_a, up_b, low_a, low_b,
    out_ref, trace_ref, band, full, sq, fmask, cube, sems,
):
    height, half = own_a.shape
    block_rows = height // BLK
    slots = 2 * half // BLK
    col = col_ref[0]
    mine = pl.multiple_of(col * half, half)
    other = pl.multiple_of((1 - col) * half, half)
    copies = []
    for k, (src, row, lane) in enumerate((
        (own_a, 1, mine), (own_b, 1, other), (up_a, 0, mine),
        (up_b, 0, other), (low_a, 2, mine), (low_b, 2, other),
    )):
        copy = pltpu.make_async_copy(
            src, band.at[pl.ds(row * height, height), pl.ds(lane, half)], sems.at[k]
        )
        copy.start()
        copies.append(copy)
    width = full.shape[1]
    wide = spread(filter_ref[...], slots * BLK)
    for i in range(block_rows):
        fmask[pl.ds(i, 1), :] = placed(wide[i : i + 1], i * BLK, width)

    def skew(row):
        for r in range(row * block_rows, (row + 1) * block_rows):
            rows = band[pl.ds(r * BLK, BLK), :]
            full[pl.ds(r * BLK, BLK), :] = placed(rows, (r - block_rows) * BLK, width)

    copies[0].wait()
    copies[1].wait()
    skew(1)
    trace_ref[...] = jnp.zeros_like(trace_ref)
    trace_ref[pl.ds(0, 1), :] = eye_sum(full.at[pl.ds(height, height), :], height)
    copies[2].wait()
    copies[3].wait()
    skew(0)
    copies[4].wait()
    copies[5].wait()
    skew(2)
    tiles = height // TILE
    span = (block_rows * 2 + TILE // BLK - 1) * BLK
    span = -(-span // TILE)
    reach = height // TILE
    per_tile = TILE // BLK
    sq[...] = jnp.zeros_like(sq)
    for m in range(tiles):
        for b in range(m, m + span):
            first = max(b - reach, m)
            last = min(b + reach, m + span - 1)
            k0, klen = first * TILE, (last - first + 1) * TILE
            prod = jnp.dot(
                full[pl.ds(height + m * TILE, TILE), pl.ds(k0, klen)],
                full[pl.ds(k0, klen), pl.ds(b * TILE, TILE)],
                preferred_element_type=jnp.float32,
            )
            for i in range(per_tile):
                row = m * per_tile + i
                keep = fmask[pl.ds(row, 1), pl.ds(b * TILE, TILE)]
                sq[pl.ds(row * BLK, BLK), pl.ds(b * TILE, TILE)] = (
                    prod[i * BLK : (i + 1) * BLK] * keep
                ).astype(jnp.bfloat16)
    trace_ref[pl.ds(1, 1), :] = eye_sum(sq, height)
    out_span = half // TILE + 1
    for m in range(tiles):
        lanes = pl.multiple_of(m * TILE + col * half, TILE)
        cube[...] = jnp.dot(
            sq[pl.ds(m * TILE, TILE), pl.ds(m * TILE, span * TILE)],
            full[pl.ds(m * TILE, span * TILE), pl.ds(lanes, out_span * TILE)],
            preferred_element_type=jnp.float32,
        )
        for i in range(per_tile):
            row = m * per_tile + i
            base = i * BLK // LANES * LANES
            shift = i * BLK - base
            size = half + (LANES if shift else 0)
            at = pl.ds(pl.multiple_of(m * TILE + base + col * half, LANES), size)
            kept = sq[pl.ds(row * BLK, BLK), at].astype(jnp.float32)
            keep = fmask[pl.ds(row, 1), at]
            part = cube[pl.ds(i * BLK, BLK), pl.ds(base, size)]
            result = (3.0 * kept - 2.0 * (part * keep)).astype(jnp.bfloat16)
            out_ref[pl.ds(row * BLK, BLK), :] = result[:, shift : shift + half]


def purify(col, keep_filter, *pieces):
    height, half = pieces[0].shape
    width = 3 * height
    block_rows = height // BLK
    anywhere = pl.BlockSpec(memory_space=pl.ANY)
    vmem = pl.BlockSpec(memory_space=pltpu.VMEM)
    return pl.pallas_call(
        purify_kernel,
        out_shape=(
            jax.ShapeDtypeStruct((height, half), jnp.bfloat16),
            jax.ShapeDtypeStruct((8, LANES), jnp.float32),
        ),
        in_specs=[pl.BlockSpec(memory_space=pltpu.SMEM), vmem] + [anywhere] * 6,
        out_specs=(vmem, vmem),
        scratch_shapes=[
            pltpu.VMEM((width, 2 * half), jnp.bfloat16),
            pltpu.VMEM((width, width), jnp.bfloat16),
            pltpu.VMEM((height, width), jnp.bfloat16),
            pltpu.VMEM((block_rows, width), jnp.float32),
            pltpu.VMEM((TILE, half + TILE), jnp.float32),
            pltpu.SemaphoreType.DMA((6,)),
        ],
        compiler_params=pltpu.CompilerParams(vmem_limit_bytes=48 * 1024 * 1024),
        cost_estimate=pl.CostEstimate(flops=3 * 10**9, bytes_accessed=4 * 10**6, transcendentals=0),
        name="purify",
    )(col, keep_filter, *pieces)


def valid_slots(first_row, row_count, first_slot, slot_count, half_band, block_total):
    row_index = first_row + jnp.arange(row_count, dtype=jnp.int32)
    slot_index = first_slot + jnp.arange(slot_count, dtype=jnp.int32)
    column_index = row_index[:, None] + slot_index[None, :] - half_band
    return ((column_index >= 0) & (column_index < block_total)).astype(jnp.int32)


def expand_mask(values, keep_mask):
    block_rows, slot_count = keep_mask.shape
    blocks = values.reshape(block_rows, BLK, slot_count, BLK)
    blocks = blocks * keep_mask.astype(values.dtype)[:, None, :, None]
    return blocks.reshape(block_rows * BLK, slot_count * BLK)


def swapped(value):
    return lax.ppermute(value, "col", [(0, 1), (1, 0)])


def per_device(density, pattern, filter_mask):
    half_slots = density.shape[1] // BLK
    slot_count = 2 * half_slots
    block_rows = density.shape[0] // BLK
    col = lax.axis_index("col")
    row = lax.axis_index("row")
    size = lax.axis_size("row")
    block_total = block_rows * size
    valid = valid_slots(row * block_rows, block_rows, 0, slot_count, half_slots, block_total)
    own_valid = lax.dynamic_slice_in_dim(valid, col * half_slots, half_slots, 1)
    kept = expand_mask(density, pattern * own_valid)
    up = lax.ppermute(kept, "row", [(i, (i + 1) % size) for i in range(size)])
    low = lax.ppermute(kept, "row", [((i + 1) % size, i) for i in range(size)])
    own_b = swapped(kept)
    up_b, low_b = swapped(up), swapped(low)
    purified, sums = purify(
        col.reshape(1).astype(jnp.int32), filter_mask * valid, kept, own_b, up, up_b, low, low_b
    )
    sums = jnp.sum(sums[:2], axis=1)
    spread_sums = jnp.zeros((1, LANES), jnp.float32).at[0, :2].set(sums)
    copies = jnp.broadcast_to(spread_sums[None], (size, 1, LANES))
    copies = lax.all_to_all(copies, "row", split_axis=0, concat_axis=0, tiled=True)
    traces = jnp.sum(copies, axis=(0, 1))[:2] / (block_total * BLK)
    return purified, traces


def solution(mesh):
    placed_as = (P(SNAP_ROW, "col"), P(SNAP_ROW, "col"), P(SNAP_ROW, None))
    return jax.shard_map(
        per_device,
        mesh=mesh,
        in_specs=placed_as,
        out_specs=(P(SNAP_ROW, "col"), P("snap")),
        check_vma=False,
    )
```

time: 569 us -> 102 us (0.18)
  local copies, waits for them, and re-layouts: 379 us -> 2.45 us
  blocking collectives: 99.3 us -> 24.9 us
  starting transfers between devices: 3.92 us -> 57.7 us
  matrix products: 23.9 us -> 0 us
  other arithmetic: 22.8 us -> 3.14 us
  between operations: 14.2 us -> 0.77 us
  loops' own time: 12.5 us -> 0 us
    while x409 -> x0, local copies, waits for them, and re-layouts: 183 us -> none
    slice x120 -> x0, local copies, waits for them, and re-layouts: 87 us -> none  [shift_slots(): segment[:, :segment.shape[1] - moved * BLK]]
    dynamic_slice x156 -> x0, local copies, waits for them, and re-layouts: 62 us -> none  [the longest x136 41.9 us: one_group(): lax.dynamic_slice_in_dim(segment, first_slot * BLK, column_slots * BLK, 1)]
    ppermute x2 -> x5, starting transfers between devices: 3.86 us -> 57.7 us  [the longest x1 45.7 us: per_device(): low = lax.ppermute(kept, 'row', [((i + 1) % size, i) for i in range(size)])]
    psum x3 -> x0, blocking collectives: 53.6 us -> none  [over_axes(): return functools.reduce(lax.psum, axes, value)]
    dot_general x8 -> x0, matrix products: 23.9 us -> none  [one_group(): jnp.einsum('gak,gkn->gan', left_rows, gathered, preferred_element_type=jn...]
    all_to_all x1, blocking collectives: 45.6 us -> 24.9 us  [per_device(): lax.all_to_all(copies, 'row', split_axis=0, concat_axis=0, tiled=True)]
    another operation x12 -> x0, local copies, waits for them, and re-layouts: 18.7 us -> none  [the longest x2 11.1 us: expand_mask(): blocks = values.reshape(block_rows, BLK, slot_count, BLK)]
  transfers between devices with their start and end apart: 3 -> 5, of which waited for: 2 -> 2; matrix products, arithmetic and copies ran while one was open for 8% -> 1% of each run, Pallas kernels for 0% -> 0%
where the time goes in v1:
time: 102 us
  starting transfers between devices  57.7 us (57%)
  blocking collectives  24.9 us (24%)
  waiting for transfers between devices  7.96 us (8%)
  Pallas kernels  4.78 us (5%)
  other arithmetic  3.14 us (3%)
  local copies, waits for them, and re-layouts  2.45 us (2%)
    ppermute x1, starting transfers between devices, per_device(): low = lax.ppermute(kept, 'row', [((i + 1) % size, i) for i in range(size)])  45.7 us
    all_to_all x1, blocking collectives, per_device(): lax.all_to_all(copies, 'row', split_axis=0, concat_axis=0, tiled=True)  24.9 us
    ppermute x3, starting transfers between devices, swapped(): return lax.ppermute(value, 'col', [(0, 1), (1, 0)])  7.89 us
    ppermute x1, waiting for transfers between devices, per_device(): up = lax.ppermute(kept, 'row', [(i, (i + 1) % size) for i in range(size)])  6.88 us
    pallas_call x1, Pallas kernels, purify(): pl.pallas_call(purify_kernel, out_shape=(jax.ShapeDtypeStruct((height, ha...  4.78 us
    ppermute x1, starting transfers between devices, per_device(): up = lax.ppermute(kept, 'row', [(i, (i + 1) % size) for i in range(size)])  4.1 us
    mul x2, local copies, waits for them, and re-layouts, expand_mask(): blocks = blocks * keep_mask.astype(values.dtype)[:, None, :, None]  2.4 us
  transfers between devices with their start and end apart: 5, of which 2 were waited for; matrix products, arithmetic and copies ran while one was open for 1% of the time, Pallas kernels for 0%

profile of v1, /device:TPU:65, one launch (start us, length us, event | category | flops | bytes accessed | tf_op | source)
XLA Modules:
  0.0 101.7 jit_solution(11469184209040289814)
XLA Ops:
  0.6 0.1 fusion.2
  0.7 0.8 multiply_convert_fusion
  1.5 0.0 copy-start
  1.5 0.3 mul.27
  1.8 0.0 copy-start.1
  1.9 2.1 %mul.28 = bf16[512,512]{1,0:T(8,128)(2,1)S(1)} reshape(bf16[16,32,16,32]{3,2,1,0:T(8,128)(2,1)S(1)} %mul.27) | data formatting | bytes 1048576 | tf_op jit(solution)/shard_map/mul | solution.py:178
  3.9 0.0 copy-done
  3.9 0.1 mul.29.own_a
  4.1 4.1 %collective-permute-start.1 = (bf16[512,512]{1,0:T(8,128)(2,1)S(1)}, bf16[512,512]{1,0:T(8,128)(2,1)S(1)}, u32[]{:S(2)}, u32[]{:S(2)}) collective-permute-start(bf16[512,512]{1,0:T(8,128)(2,1)S(1)} %mul.29.own_a), channel_id=1, source_target_pairs={{0,2},{2,4},{4,6},{6,8},{8,10},{10,12},{12,14},{14,16},{16,18},{18... | collective-permute-start | bytes 1572872 | tf_op jit(solution)/shard_map/ppermute | solution.py:197
  8.2 45.7 %collective-permute-start.3 = (bf16[512,512]{1,0:T(8,128)(2,1)S(1)}, bf16[512,512]{1,0:T(8,128)(2,1)S(1)}, u32[]{:S(2)}, u32[]{:S(2)}) collective-permute-start(bf16[512,512]{1,0:T(8,128)(2,1)S(1)} %mul.29.own_a), channel_id=1, source_target_pairs={{2,0},{4,2},{6,4},{8,6},{10,8},{12,10},{14,12},{16,14},{18,16},{20... | collective-permute-start | bytes 1572872 | tf_op jit(solution)/shard_map/ppermute | solution.py:198
  53.9 2.8 %collective-permute-start = (bf16[512,512]{1,0:T(8,128)(2,1)S(1)}, bf16[512,512]{1,0:T(8,128)(2,1)S(1)}, u32[]{:S(2)}, u32[]{:S(2)}) collective-permute-start(bf16[512,512]{1,0:T(8,128)(2,1)S(1)} %mul.29.own_a), channel_id=1, source_target_pairs={{0,1},{1,0},{2,3},{3,2},{4,5},{5,4},{6,7},{7,6},{8,9},{9,8},{10,11... | collective-permute-start | bytes 1572872 | tf_op jit(solution)/shard_map/ppermute | solution.py:183
  56.7 6.9 %collective-permute-done.1.up_a = bf16[512,512]{1,0:T(8,128)(2,1)S(1)} collective-permute-done((bf16[512,512]{1,0:T(8,128)(2,1)S(1)}, bf16[512,512]{1,0:T(8,128)(2,1)S(1)}, u32[]{:S(2)}, u32[]{:S(2)}) %collective-permute-start.1) | collective-permute-done | bytes 524320 | tf_op jit(solution)/shard_map/ppermute | solution.py:197
  63.6 3.1 %collective-permute-start.2 = (bf16[512,512]{1,0:T(8,128)(2,1)S(1)}, bf16[512,512]{1,0:T(8,128)(2,1)S(1)}, u32[]{:S(2)}, u32[]{:S(2)}) collective-permute-start(bf16[512,512]{1,0:T(8,128)(2,1)S(1)} %collective-permute-done.1.up_a), channel_id=1, source_target_pairs={{0,1},{1,0},{2,3},{3,2},{4,5},{5,4},{6,7},{7,6},{8,9},{9,8},{10,11... | collective-permute-start | bytes 1572872 | tf_op jit(solution)/shard_map/ppermute | solution.py:183
  66.7 0.0 collective-permute-done.3.low_a
  66.7 2.0 %collective-permute-start.4 = (bf16[512,512]{1,0:T(8,128)(2,1)S(1)}, bf16[512,512]{1,0:T(8,128)(2,1)S(1)}, u32[]{:S(2)}, u32[]{:S(2)}) collective-permute-start(bf16[512,512]{1,0:T(8,128)(2,1)S(1)} %collective-permute-done.3.low_a), channel_id=1, source_target_pairs={{0,1},{1,0},{2,3},{3,2},{4,5},{5,4},{6,7},{7,6},{8,9},{9,8},{10,11... | collective-permute-start | bytes 1572872 | tf_op jit(solution)/shard_map/ppermute | solution.py:183
  68.7 0.7 compare_reduce_fusion
  69.4 0.0 copy-done.1
  69.4 0.1 broadcast_select_fusion.filter_ref
  69.5 0.0 collective-permute-done.own_b
  69.5 0.0 collective-permute-done.2.up_b
  69.5 1.1 %collective-permute-done.4.low_b = bf16[512,512]{1,0:T(8,128)(2,1)S(1)} collective-permute-done((bf16[512,512]{1,0:T(8,128)(2,1)S(1)}, bf16[512,512]{1,0:T(8,128)(2,1)S(1)}, u32[]{:S(2)}, u32[]{:S(2)}) %collective-permute-start.4) | collective-permute-done | bytes 524320 | tf_op jit(solution)/shard_map/ppermute | solution.py:183
  70.5 4.8 %purify.1 = (bf16[512,512]{1,0:T(8,128)(2,1)}, f32[8,128]{1,0:T(8,128)S(1)}) custom-call(s32[1]{0:T(128)} %bitcast.col_ref, s32[16,32]{1,0:T(8,128)S(1)} %broadcast_select_fusion.filter_ref, bf16[512,512]{1,0:T(8,128)(2,1)S(1)} %mul.29.own_a, bf16[512,512]{1,0:T(8,128)(2,1)S(1)} %collective-permute-done.own_b, ...), custom_call_target="tpu_custom_call" | custom-call | flops 3000000000 | bytes 4000000 | tf_op jit(solution)/shard_map/purify/pallas_call | solution.py:146
  75.3 0.1 slice_reduce_fusion
  75.5 0.7 broadcast_select_fusion.1
  76.2 24.9 %all_to_all.5 = f32[128,1,128]{2,1,0:T(1,128)S(1)} all-to-all(f32[128,1,128]{2,1,0:T(1,128)S(1)} %broadcast_in_dim.5), channel_id=1, replica_groups=mesh['snap'=2,'row'=128,'col'=2] {'row'}, dimensions={0} | all-to-all | bytes 131072 | tf_op jit(solution)/shard_map/all_to_all | solution.py:207
  101.1 0.5 slice_multiply_fusion
  (4 shorter events, 0.1 us)
Async XLA Ops:
  1.5 2.4 %copy-start = (bf16[512,512]{1,0:T(8,128)(2,1)S(1)}, bf16[512,512]{1,0:T(8,128)(2,1)}, u32[]{:S(2)}) copy-start(bf16[512,512]{1,0:T(8,128)(2,1)} %param.5) | copy-start | bytes 1572868
  1.8 67.5 %copy-start.1 = (s32[16,32]{1,0:T(8,128)S(1)}, s32[16,32]{1,0:T(8,128)}, u32[]{:S(2)}) copy-start(s32[16,32]{1,0:T(8,128)} %param.7) | copy-start | bytes 6148
  4.1 59.5 %collective-permute-start.1 = (bf16[512,512]{1,0:T(8,128)(2,1)S(1)}, bf16[512,512]{1,0:T(8,128)(2,1)S(1)}, u32[]{:S(2)}, u32[]{:S(2)}) collective-permute-start(bf16[512,512]{1,0:T(8,128)(2,1)S(1)} %mul.29.own_a), channel_id=1, source_target_pairs={{0,2},{2,4},{4,6},{6,8},{8,10},{10,12},{12,14},{14,16},{16,18},{18... | collective-permute-start | bytes 1572872 | tf_op jit(solution)/shard_map/ppermute | solution.py:197
  8.2 58.5 %collective-permute-start.3 = (bf16[512,512]{1,0:T(8,128)(2,1)S(1)}, bf16[512,512]{1,0:T(8,128)(2,1)S(1)}, u32[]{:S(2)}, u32[]{:S(2)}) collective-permute-start(bf16[512,512]{1,0:T(8,128)(2,1)S(1)} %mul.29.own_a), channel_id=1, source_target_pairs={{2,0},{4,2},{6,4},{8,6},{10,8},{12,10},{14,12},{16,14},{18,16},{20... | collective-permute-start | bytes 1572872 | tf_op jit(solution)/shard_map/ppermute | solution.py:198
  53.9 15.6 %collective-permute-start = (bf16[512,512]{1,0:T(8,128)(2,1)S(1)}, bf16[512,512]{1,0:T(8,128)(2,1)S(1)}, u32[]{:S(2)}, u32[]{:S(2)}) collective-permute-start(bf16[512,512]{1,0:T(8,128)(2,1)S(1)} %mul.29.own_a), channel_id=1, source_target_pairs={{0,1},{1,0},{2,3},{3,2},{4,5},{5,4},{6,7},{7,6},{8,9},{9,8},{10,11... | collective-permute-start | bytes 1572872 | tf_op jit(solution)/shard_map/ppermute | solution.py:183
  63.6 5.9 %collective-permute-start.2 = (bf16[512,512]{1,0:T(8,128)(2,1)S(1)}, bf16[512,512]{1,0:T(8,128)(2,1)S(1)}, u32[]{:S(2)}, u32[]{:S(2)}) collective-permute-start(bf16[512,512]{1,0:T(8,128)(2,1)S(1)} %collective-permute-done.1.up_a), channel_id=1, source_target_pairs={{0,1},{1,0},{2,3},{3,2},{4,5},{5,4},{6,7},{7,6},{8,9},{9,8},{10,11... | collective-permute-start | bytes 1572872 | tf_op jit(solution)/shard_map/ppermute | solution.py:183
  66.7 3.8 %collective-permute-start.4 = (bf16[512,512]{1,0:T(8,128)(2,1)S(1)}, bf16[512,512]{1,0:T(8,128)(2,1)S(1)}, u32[]{:S(2)}, u32[]{:S(2)}) collective-permute-start(bf16[512,512]{1,0:T(8,128)(2,1)S(1)} %collective-permute-done.3.low_a), channel_id=1, source_target_pairs={{0,1},{1,0},{2,3},{3,2},{4,5},{5,4},{6,7},{7,6},{8,9},{9,8},{10,11... | collective-permute-start | bytes 1572872 | tf_op jit(solution)/shard_map/ppermute | solution.py:183

commit v2 on v1

--- a/solution.py
+++ b/solution.py
@@ -1,11 +1,10 @@
-import functools
-
 import jax
 import jax.numpy as jnp
 from jax import lax
 from jax.experimental import pallas as pl
 from jax.experimental.pallas import tpu as pltpu
 from jax.sharding import PartitionSpec as P
+
 
 BLK = 32
 LANES = 128
@@ -52,28 +51,184 @@
     return total
 
 
+def own_valid(scalars, block_rows, first_slot, slots, half_band):
+    row = lax.broadcasted_iota(jnp.int32, (block_rows, slots), 0)
+    slot = lax.broadcasted_iota(jnp.int32, (block_rows, slots), 1)
+    column = scalars[1] + row + first_slot + slot - half_band
+    return (column >= 0) & (column < scalars[2])
+
+
+def keep_kernel(scalars, density, pattern, keep_filter, kept):
+    height, half = density.shape
+    block_rows, slots = pattern.shape
+    valid = own_valid(scalars, block_rows, scalars[0] * slots, slots, slots)
+    mask = spread(jnp.where(valid, pattern[...], 0), half).astype(jnp.bfloat16)
+    for i in range(block_rows):
+        rows = pl.ds(i * BLK, BLK)
+        kept[rows, :] = density[rows, :] * mask[i : i + 1]
+    slot = lax.broadcasted_iota(jnp.int32, keep_filter.shape, 1)
+    on_diagonal = jnp.where(slot == slots, keep_filter[...], 0).astype(jnp.float32)
+    on_diagonal = jnp.sum(on_diagonal, axis=1, keepdims=True)
+    kept[pl.ds(height, block_rows), :] = jnp.broadcast_to(
+        on_diagonal, (block_rows, half)
+    ).astype(jnp.bfloat16)
+
+
+def keep(scalars, density, pattern, keep_filter):
+    height, half = density.shape
+    vmem = pl.BlockSpec(memory_space=pltpu.VMEM)
+    return pl.pallas_call(
+        keep_kernel,
+        out_shape=jax.ShapeDtypeStruct((height + pattern.shape[0], half), jnp.bfloat16),
+        in_specs=[pl.BlockSpec(memory_space=pltpu.SMEM), vmem, vmem, vmem],
+        out_specs=vmem,
+        compiler_params=pltpu.CompilerParams(vmem_limit_bytes=16 * 1024 * 1024),
+        cost_estimate=pl.CostEstimate(flops=10**9, bytes_accessed=10**6, transcendentals=0),
+        name="keep",
+    )(scalars, density, pattern, keep_filter)
+
+
+def joined(left, right):
+    parts = [part for part in (left, right) if part.shape[1]]
+    return jnp.concatenate(parts, 1) if len(parts) > 1 else parts[0]
+
+
+def weighted_diagonal(a, b, weight):
+    total = jnp.zeros((1, TILE), jnp.float32)
+    row = lax.broadcasted_iota(jnp.int32, (TILE, TILE), 0)
+    lane = lax.broadcasted_iota(jnp.int32, (TILE, TILE), 1)
+    for m in range(a.shape[0] // TILE):
+        at = pl.ds(m * TILE, TILE)
+        prod = jnp.dot(a[at, :], b[:, at], preferred_element_type=jnp.float32)
+        diagonal = jnp.sum(jnp.where(row == lane, prod, 0.0), axis=0, keepdims=True)
+        total += diagonal * weight[:, m * TILE : (m + 1) * TILE]
+    return jnp.sum(total)
+
+
+def trace_kernel(
+    scalars, own_a, own_b, near, out_ref, left, right, upper, lower, square, x_ref, y_ref, sems
+):
+    half = own_a.shape[1]
+    height = square.shape[0]
+    block_rows = height // BLK
+    col = scalars[0]
+
+    def fetch(sources):
+        copies = [
+            pltpu.make_async_copy(src, dst, sems.at[k])
+            for k, (src, dst) in enumerate(zip(sources, (left, right, upper, lower)))
+        ]
+        for copy in copies:
+            copy.start()
+        for copy in copies:
+            copy.wait()
+
+    @pl.when(col == 0)
+    def _():
+        fetch((own_a, own_b, near, own_a))
+
+    @pl.when(col != 0)
+    def _():
+        fetch((own_b, own_a, own_a, near))
+
+    for i in range(block_rows):
+        rows = pl.ds(i * BLK, BLK)
+        cut = half - i * BLK
+        square[rows, :] = joined(left[rows, :][:, cut:], right[rows, :][:, :cut])
+        gap = jnp.zeros((BLK, cut), jnp.bfloat16)
+        x_ref[rows, :] = joined(upper[rows, :][:, cut:], gap)
+        gap = jnp.zeros((BLK, half - cut), jnp.bfloat16)
+        y_ref[rows, :] = joined(gap, lower[rows, :][:, :cut])
+    block = lax.broadcasted_iota(jnp.int32, (block_rows, half), 0)
+    lane = lax.broadcasted_iota(jnp.int32, (block_rows, half), 1) // BLK
+
+    def weight(ref):
+        values = ref[pl.ds(height, block_rows), :].astype(jnp.float32)
+        return jnp.sum(jnp.where(block == lane, values, 0.0), axis=0, keepdims=True)
+
+    kept = jnp.sum(eye_sum(square, 0))
+    own = weighted_diagonal(square, square, weight(left))
+    across = weighted_diagonal(x_ref, y_ref, weight(upper))
+    across += weighted_diagonal(y_ref, x_ref, weight(lower))
+    lane = lax.broadcasted_iota(jnp.int32, out_ref.shape, 2)
+    out_ref[...] = jnp.where(lane == 0, kept, jnp.where(lane == 1, own, across))
+
+
+def partial_traces(scalars, own_a, own_b, near, copies):
+    rows, half = own_a.shape
+    anywhere = pl.BlockSpec(memory_space=pl.ANY)
+    return pl.pallas_call(
+        trace_kernel,
+        out_shape=jax.ShapeDtypeStruct((copies, 1, LANES), jnp.float32),
+        in_specs=[pl.BlockSpec(memory_space=pltpu.SMEM)] + [anywhere] * 3,
+        out_specs=pl.BlockSpec(memory_space=pltpu.VMEM),
+        scratch_shapes=[pltpu.VMEM((rows, half), jnp.bfloat16)] * 4
+        + [pltpu.VMEM((half, half), jnp.bfloat16)] * 3
+        + [pltpu.SemaphoreType.DMA((4,))],
+        compiler_params=pltpu.CompilerParams(vmem_limit_bytes=24 * 1024 * 1024),
+        cost_estimate=pl.CostEstimate(flops=10**9, bytes_accessed=2 * 10**6, transcendentals=0),
+        name="partial_traces",
+    )(scalars, own_a, own_b, near)
+
+
+def total_kernel(scalars, sums, out_ref):
+    values = sums[:, 0, :]
+    moved = pltpu.roll(values, values.shape[0] - 1, 0)
+    moved = jnp.where(scalars[0] == 0, moved, values)
+    lane = lax.broadcasted_iota(jnp.int32, (1, LANES), 1)
+    total = jnp.sum(values, axis=0, keepdims=True)
+    across = jnp.sum(moved, axis=0, keepdims=True)
+    order = (scalars[2] * BLK).astype(jnp.float32)
+
+    def pick(row, k):
+        return jnp.sum(jnp.where(lane == k, row, 0.0))
+
+    out_ref[0] = pick(total, 0) / order
+    out_ref[1] = (pick(total, 1) + pick(across, 2)) / order
+
+
+def total(scalars, sums):
+    return pl.pallas_call(
+        total_kernel,
+        out_shape=jax.ShapeDtypeStruct((2,), jnp.float32),
+        in_specs=[
+            pl.BlockSpec(memory_space=pltpu.SMEM),
+            pl.BlockSpec(memory_space=pltpu.VMEM),
+        ],
+        out_specs=pl.BlockSpec(memory_space=pltpu.SMEM),
+        compiler_params=pltpu.CompilerParams(vmem_limit_bytes=8 * 1024 * 1024),
+        name="total",
+    )(scalars, sums)
+
+
 def purify_kernel(
-    col_ref, filter_ref, own_a, own_b, up_a, up_b, low_a, low_b,
-    out_ref, trace_ref, band, full, sq, fmask, cube, sems,
+    scalars, filter_ref, own_a, own_b, near, near_b, far, far_b,
+    out_ref, band, full, sq, fmask, cube, sems,
 ):
-    height, half = own_a.shape
+    height, half = out_ref.shape
     block_rows = height // BLK
     slots = 2 * half // BLK
-    col = col_ref[0]
+    col = scalars[0]
     mine = pl.multiple_of(col * half, half)
     other = pl.multiple_of((1 - col) * half, half)
+    inner = 2 * col
+    places = (
+        (own_a, 1, mine), (own_b, 1, other), (near, inner, other),
+        (near_b, 2 - inner, mine), (far, 2 - inner, other), (far_b, inner, mine),
+    )
     copies = []
-    for k, (src, row, lane) in enumerate((
-        (own_a, 1, mine), (own_b, 1, other), (up_a, 0, mine),
-        (up_b, 0, other), (low_a, 2, mine), (low_b, 2, other),
-    )):
+    for k, (src, row, lane) in enumerate(places):
+        start = pl.multiple_of(row * height, height)
         copy = pltpu.make_async_copy(
-            src, band.at[pl.ds(row * height, height), pl.ds(lane, half)], sems.at[k]
+            src.at[pl.ds(0, height), :],
+            band.at[pl.ds(start, height), pl.ds(lane, half)],
+            sems.at[k],
         )
         copy.start()
         copies.append(copy)
     width = full.shape[1]
-    wide = spread(filter_ref[...], slots * BLK)
+    valid = own_valid(scalars, block_rows, 0, slots, slots // 2)
+    wide = spread(jnp.where(valid, filter_ref[...], 0), slots * BLK)
     for i in range(block_rows):
         fmask[pl.ds(i, 1), :] = placed(wide[i : i + 1], i * BLK, width)
 
@@ -85,13 +240,9 @@
     copies[0].wait()
     copies[1].wait()
     skew(1)
-    trace_ref[...] = jnp.zeros_like(trace_ref)
-    trace_ref[pl.ds(0, 1), :] = eye_sum(full.at[pl.ds(height, height), :], height)
-    copies[2].wait()
-    copies[3].wait()
+    for copy in copies[2:]:
+        copy.wait()
     skew(0)
-    copies[4].wait()
-    copies[5].wait()
     skew(2)
     tiles = height // TILE
     span = (block_rows * 2 + TILE // BLK - 1) * BLK
@@ -115,7 +266,6 @@
                 sq[pl.ds(row * BLK, BLK), pl.ds(b * TILE, TILE)] = (
                     prod[i * BLK : (i + 1) * BLK] * keep
                 ).astype(jnp.bfloat16)
-    trace_ref[pl.ds(1, 1), :] = eye_sum(sq, height)
     out_span = half // TILE + 1
     for m in range(tiles):
         lanes = pl.multiple_of(m * TILE + col * half, TILE)
@@ -137,20 +287,17 @@
             out_ref[pl.ds(row * BLK, BLK), :] = result[:, shift : shift + half]
 
 
-def purify(col, keep_filter, *pieces):
-    height, half = pieces[0].shape
+def purify(scalars, keep_filter, height, *pieces):
+    half = pieces[0].shape[1]
     width = 3 * height
     block_rows = height // BLK
     anywhere = pl.BlockSpec(memory_space=pl.ANY)
     vmem = pl.BlockSpec(memory_space=pltpu.VMEM)
     return pl.pallas_call(
         purify_kernel,
-        out_shape=(
-            jax.ShapeDtypeStruct((height, half), jnp.bfloat16),
-            jax.ShapeDtypeStruct((8, LANES), jnp.float32),
-        ),
+        out_shape=jax.ShapeDtypeStruct((height, half), jnp.bfloat16),
         in_specs=[pl.BlockSpec(memory_space=pltpu.SMEM), vmem] + [anywhere] * 6,
-        out_specs=(vmem, vmem),
+        out_specs=vmem,
         scratch_shapes=[
             pltpu.VMEM((width, 2 * half), jnp.bfloat16),
             pltpu.VMEM((width, width), jnp.bfloat16),
@@ -162,51 +309,37 @@
         compiler_params=pltpu.CompilerParams(vmem_limit_bytes=48 * 1024 * 1024),
         cost_estimate=pl.CostEstimate(flops=3 * 10**9, bytes_accessed=4 * 10**6, transcendentals=0),
         name="purify",
-    )(col, keep_filter, *pieces)
-
-
-def valid_slots(first_row, row_count, first_slot, slot_count, half_band, block_total):
-    row_index = first_row + jnp.arange(row_count, dtype=jnp.int32)
-    slot_index = first_slot + jnp.arange(slot_count, dtype=jnp.int32)
-    column_index = row_index[:, None] + slot_index[None, :] - half_band
-    return ((column_index >= 0) & (column_index < block_total)).astype(jnp.int32)
-
-
-def expand_mask(values, keep_mask):
-    block_rows, slot_count = keep_mask.shape
-    blocks = values.reshape(block_rows, BLK, slot_count, BLK)
-    blocks = blocks * keep_mask.astype(values.dtype)[:, None, :, None]
-    return blocks.reshape(block_rows * BLK, slot_count * BLK)
-
-
-def swapped(value):
-    return lax.ppermute(value, "col", [(0, 1), (1, 0)])
+    )(scalars, keep_filter, *pieces)
 
 
 def per_device(density, pattern, filter_mask):
-    half_slots = density.shape[1] // BLK
-    slot_count = 2 * half_slots
-    block_rows = density.shape[0] // BLK
-    col = lax.axis_index("col")
-    row = lax.axis_index("row")
+    block_rows = pattern.shape[0]
     size = lax.axis_size("row")
-    block_total = block_rows * size
-    valid = valid_slots(row * block_rows, block_rows, 0, slot_count, half_slots, block_total)
-    own_valid = lax.dynamic_slice_in_dim(valid, col * half_slots, half_slots, 1)
-    kept = expand_mask(density, pattern * own_valid)
-    up = lax.ppermute(kept, "row", [(i, (i + 1) % size) for i in range(size)])
-    low = lax.ppermute(kept, "row", [((i + 1) % size, i) for i in range(size)])
+    row, col = lax.axis_index("row"), lax.axis_index("col")
+    scalars = jnp.stack([col, row * block_rows, size * block_rows * jnp.ones_like(row)]).astype(jnp.int32)
+    kept = keep(scalars, density, pattern, filter_mask)
+
+    def device(row, col):
+        return 2 * row + col
+
+    def exchanged(value, upper_col):
+        pairs = [
+            (device(i, upper_col), device(i + 1, 1 - upper_col)) for i in range(size - 1)
+        ]
+        return lax.ppermute(value, ("row", "col"), pairs + [(b, a) for a, b in pairs])
+
+    def swapped(value):
+        return lax.ppermute(value, "col", [(0, 1), (1, 0)])
+
+    near = exchanged(kept, 1)
     own_b = swapped(kept)
-    up_b, low_b = swapped(up), swapped(low)
-    purified, sums = purify(
-        col.reshape(1).astype(jnp.int32), filter_mask * valid, kept, own_b, up, up_b, low, low_b
-    )
-    sums = jnp.sum(sums[:2], axis=1)
-    spread_sums = jnp.zeros((1, LANES), jnp.float32).at[0, :2].set(sums)
-    copies = jnp.broadcast_to(spread_sums[None], (size, 1, LANES))
-    copies = lax.all_to_all(copies, "row", split_axis=0, concat_axis=0, tiled=True)
-    traces = jnp.sum(copies, axis=(0, 1))[:2] / (block_total * BLK)
-    return purified, traces
+    far = exchanged(kept, 0)
+    sums = partial_traces(scalars, kept, own_b, near, size)
+    sums = lax.all_to_all(sums, "row", split_axis=0, concat_axis=0, tiled=True)
+    near_b = swapped(near)
+    far_b = swapped(far)
+    purified = purify(scalars, filter_mask, density.shape[0], kept, own_b, near, near_b, far, far_b)
+    return purified, total(scalars, sums)
 
 
 def solution(mesh):

time: 102 us -> 100 us (0.980)
  waiting for transfers between devices: 7.96 us -> 0.01 us
  blocking collectives: 24.9 us -> 32.4 us
  Pallas kernels: 4.78 us -> 8.86 us
  other arithmetic: 3.14 us -> 0.08 us
  starting transfers between devices: 57.7 us -> 56 us
    ppermute x2, starting transfers between devices: 49.8 us -> 7.67 us  [exchanged(): lax.ppermute(value, ('row', 'col'), pairs + [(b, a) for a, b in pairs])]
    ppermute x3, starting transfers between devices: 7.89 us -> 48.3 us  [swapped(): return lax.ppermute(value, 'col', [(0, 1), (1, 0)])]
    all_to_all x1, blocking collectives: 24.9 us -> 32.4 us  [per_device(): sums = lax.all_to_all(sums, 'row', split_axis=0, concat_axis=0, tiled=True)]
    ppermute x2, waiting for transfers between devices: 6.89 us -> 0.01 us  [exchanged(): lax.ppermute(value, ('row', 'col'), pairs + [(b, a) for a, b in pairs])]
    pallas_call x1 -> x4, Pallas kernels: 4.78 us -> 8.86 us  [the longest x1 5.21 us: purify(): pl.pallas_call(purify_kernel, out_shape=jax.ShapeDtypeStruct((height, hal...]
    mul x2 -> x0, local copies, waits for them, and re-layouts: 2.4 us -> none  [expand_mask(): blocks = blocks * keep_mask.astype(values.dtype)[:, None, :, None]]
    unnamed x4 -> x6, local copies, waits for them, and re-layouts: 0.01 us -> 1.66 us
    ppermute x3, waiting for transfers between devices: 1.07 us -> 0.01 us  [swapped(): return lax.ppermute(value, 'col', [(0, 1), (1, 0)])]
  transfers between devices with their start and end apart: 5 -> 5, of which waited for: 2 -> 0; matrix products, arithmetic and copies ran while one was open for 1% -> 0% of each run, Pallas kernels for 0% -> 3%
where the time goes in v2:
time: 100 us; the launch traced here: 99.8 us
  starting transfers between devices  56 us (56%)
  blocking collectives  32.4 us (32%)
  Pallas kernels  8.86 us (9%)
  local copies, waits for them, and re-layouts  1.66 us (2%)
    ppermute x3, starting transfers between devices, swapped(): return lax.ppermute(value, 'col', [(0, 1), (1, 0)])  48.3 us
    all_to_all x1, blocking collectives, per_device(): sums = lax.all_to_all(sums, 'row', split_axis=0, concat_axis=0, tiled=True)  32.4 us
    ppermute x2, starting transfers between devices, exchanged(): lax.ppermute(value, ('row', 'col'), pairs + [(b, a) for a, b in pairs])  7.67 us
    pallas_call x1, Pallas kernels, purify(): pl.pallas_call(purify_kernel, out_shape=jax.ShapeDtypeStruct((height, hal...  5.21 us
  transfers between devices with their start and end apart: 5, of which 0 were waited for; matrix products, arithmetic and copies ran while one was open for 0% of the time, Pallas kernels for 3%

profile of v2, /device:TPU:65, one launch (start us, length us, event | category | flops | bytes accessed | tf_op | source)
XLA Modules:
  0.0 99.8 jit_solution(4689419786263793926)
XLA Ops:
  0.6 0.0 copy-start.2
  0.6 0.0 copy-start.1
  0.7 0.1 pad_add_fusion.scalars
  0.7 0.6 copy-done.2
  1.3 0.0 copy-done.1
  1.3 0.0 copy-start
  1.3 1.0 %copy-done = bf16[512,512]{1,0:T(8,128)(2,1)S(1)} copy-done((bf16[512,512]{1,0:T(8,128)(2,1)S(1)}, bf16[512,512]{1,0:T(8,128)(2,1)}, u32[]{:S(2)}) %copy-start) | copy-done | bytes 524312
  2.4 0.7 keep.1.own_a
  3.1 0.7 collective-permute-start.3
  3.8 7.0 %collective-permute-start.1 = (bf16[528,512]{1,0:T(8,128)(2,1)S(1)}, bf16[528,512]{1,0:T(8,128)(2,1)S(1)}, u32[]{:S(2)}, u32[]{:S(2)}) collective-permute-start(bf16[528,512]{1,0:T(8,128)(2,1)S(1)} %keep.1.own_a), channel_id=1, source_target_pairs={{1,2},{3,4},{5,6},{7,8},{9,10},{11,12},{13,14},{15,16},{17,18},{19... | collective-permute-start | bytes 1622024 | tf_op jit(solution)/shard_map/ppermute | solution.py:329
  10.8 38.3 %collective-permute-start = (bf16[528,512]{1,0:T(8,128)(2,1)S(1)}, bf16[528,512]{1,0:T(8,128)(2,1)S(1)}, u32[]{:S(2)}, u32[]{:S(2)}) collective-permute-start(bf16[528,512]{1,0:T(8,128)(2,1)S(1)} %keep.1.own_a), channel_id=1, source_target_pairs={{0,1},{1,0},{2,3},{3,2},{4,5},{5,4},{6,7},{7,6},{8,9},{9,8},{10,11... | collective-permute-start | bytes 1622024 | tf_op jit(solution)/shard_map/ppermute | solution.py:332
  49.1 0.0 collective-permute-done.3.far
  49.1 8.0 %collective-permute-start.4 = (bf16[528,512]{1,0:T(8,128)(2,1)S(1)}, bf16[528,512]{1,0:T(8,128)(2,1)S(1)}, u32[]{:S(2)}, u32[]{:S(2)}) collective-permute-start(bf16[528,512]{1,0:T(8,128)(2,1)S(1)} %collective-permute-done.3.far), channel_id=1, source_target_pairs={{0,1},{1,0},{2,3},{3,2},{4,5},{5,4},{6,7},{7,6},{8,9},{9,8},{10,11... | collective-permute-start | bytes 1622024 | tf_op jit(solution)/shard_map/ppermute | solution.py:332
  57.2 0.0 collective-permute-done.1.near
  57.2 2.0 %collective-permute-start.2 = (bf16[528,512]{1,0:T(8,128)(2,1)S(1)}, bf16[528,512]{1,0:T(8,128)(2,1)S(1)}, u32[]{:S(2)}, u32[]{:S(2)}) collective-permute-start(bf16[528,512]{1,0:T(8,128)(2,1)S(1)} %collective-permute-done.1.near), channel_id=1, source_target_pairs={{0,1},{1,0},{2,3},{3,2},{4,5},{5,4},{6,7},{7,6},{8,9},{9,8},{10,11... | collective-permute-start | bytes 1622024 | tf_op jit(solution)/shard_map/ppermute | solution.py:332
  59.1 0.0 collective-permute-done.own_b
  59.2 1.7 %partial_traces.1 = f32[128,1,128]{2,1,0:T(1,128)S(1)} custom-call(s32[3]{0:T(128)S(1)} %pad_add_fusion.scalars, bf16[528,512]{1,0:T(8,128)(2,1)S(1)} %keep.1.own_a, bf16[528,512]{1,0:T(8,128)(2,1)S(1)} %collective-permute-done.own_b, bf16[528,512]{1,0:T(8,128)(2,1)S(1)} %collective-permute-done.1.near), custom_call_target="tpu_custom_call" | custom-call | flops 1000000000 | bytes 2000000 | tf_op jit(solution)/shard_map/partial_traces/pallas_call | solution.py:160
  60.9 32.4 %all_to_all.5.sums = f32[128,1,128]{2,1,0:T(1,128)S(1)} all-to-all(f32[128,1,128]{2,1,0:T(1,128)S(1)} %partial_traces.1), channel_id=1, replica_groups=mesh['snap'=2,'row'=128,'col'=2] {'row'}, dimensions={0} | all-to-all | bytes 131072 | tf_op jit(solution)/shard_map/all_to_all | solution.py:338
  93.3 1.3 %total.1 = f32[2]{0:T(128)} custom-call(s32[3]{0:T(128)S(1)} %pad_add_fusion.scalars, f32[128,1,128]{2,1,0:T(1,128)S(1)} %all_to_all.5.sums), custom_call_target="tpu_custom_call" | custom-call | tf_op jit(solution)/shard_map/total/pallas_call | solution.py:191
  94.5 0.0 collective-permute-done.4.far_b
  94.5 0.0 collective-permute-done.2.near_b
  94.5 5.2 %purify.1 = bf16[512,512]{1,0:T(8,128)(2,1)} custom-call(s32[3]{0:T(128)S(1)} %pad_add_fusion.scalars, s32[16,32]{1,0:T(8,128)S(1)} %copy-done.2, bf16[528,512]{1,0:T(8,128)(2,1)S(1)} %keep.1.own_a, bf16[528,512]{1,0:T(8,128)(2,1)S(1)} %collective-permute-done.own_b, bf16[528,512]{1,0:T(8,128)(2,1)S(1)} %collective-permute-done.1.near, ...), custom_call_target="tpu_custom_call" | custom-call | flops 3000000000 | bytes 4000000 | tf_op jit(solution)/shard_map/purify/pallas_call | solution.py:296
Async XLA Ops:
  0.6 0.7 copy-start.2
  0.6 0.7 copy-start.1
  1.3 1.0 %copy-start = (bf16[512,512]{1,0:T(8,128)(2,1)S(1)}, bf16[512,512]{1,0:T(8,128)(2,1)}, u32[]{:S(2)}) copy-start(bf16[512,512]{1,0:T(8,128)(2,1)} %density.1) | copy-start | bytes 1572868
  3.1 46.0 %collective-permute-start.3 = (bf16[528,512]{1,0:T(8,128)(2,1)S(1)}, bf16[528,512]{1,0:T(8,128)(2,1)S(1)}, u32[]{:S(2)}, u32[]{:S(2)}) collective-permute-start(bf16[528,512]{1,0:T(8,128)(2,1)S(1)} %keep.1.own_a), channel_id=1, source_target_pairs={{0,3},{2,5},{4,7},{6,9},{8,11},{10,13},{12,15},{14,17},{16,19},{18... | collective-permute-start | bytes 1622024 | tf_op jit(solution)/shard_map/ppermute | solution.py:329
  3.8 53.4 %collective-permute-start.1 = (bf16[528,512]{1,0:T(8,128)(2,1)S(1)}, bf16[528,512]{1,0:T(8,128)(2,1)S(1)}, u32[]{:S(2)}, u32[]{:S(2)}) collective-permute-start(bf16[528,512]{1,0:T(8,128)(2,1)S(1)} %keep.1.own_a), channel_id=1, source_target_pairs={{1,2},{3,4},{5,6},{7,8},{9,10},{11,12},{13,14},{15,16},{17,18},{19... | collective-permute-start | bytes 1622024 | tf_op jit(solution)/shard_map/ppermute | solution.py:329
  10.8 48.4 %collective-permute-start = (bf16[528,512]{1,0:T(8,128)(2,1)S(1)}, bf16[528,512]{1,0:T(8,128)(2,1)S(1)}, u32[]{:S(2)}, u32[]{:S(2)}) collective-permute-start(bf16[528,512]{1,0:T(8,128)(2,1)S(1)} %keep.1.own_a), channel_id=1, source_target_pairs={{0,1},{1,0},{2,3},{3,2},{4,5},{5,4},{6,7},{7,6},{8,9},{9,8},{10,11... | collective-permute-start | bytes 1622024 | tf_op jit(solution)/shard_map/ppermute | solution.py:332
  49.1 45.4 %collective-permute-start.4 = (bf16[528,512]{1,0:T(8,128)(2,1)S(1)}, bf16[528,512]{1,0:T(8,128)(2,1)S(1)}, u32[]{:S(2)}, u32[]{:S(2)}) collective-permute-start(bf16[528,512]{1,0:T(8,128)(2,1)S(1)} %collective-permute-done.3.far), channel_id=1, source_target_pairs={{0,1},{1,0},{2,3},{3,2},{4,5},{5,4},{6,7},{7,6},{8,9},{9,8},{10,11... | collective-permute-start | bytes 1622024 | tf_op jit(solution)/shard_map/ppermute | solution.py:332
  57.2 37.4 %collective-permute-start.2 = (bf16[528,512]{1,0:T(8,128)(2,1)S(1)}, bf16[528,512]{1,0:T(8,128)(2,1)S(1)}, u32[]{:S(2)}, u32[]{:S(2)}) collective-permute-start(bf16[528,512]{1,0:T(8,128)(2,1)S(1)} %collective-permute-done.1.near), channel_id=1, source_target_pairs={{0,1},{1,0},{2,3},{3,2},{4,5},{5,4},{6,7},{7,6},{8,9},{9,8},{10,11... | collective-permute-start | bytes 1622024 | tf_op jit(solution)/shard_map/ppermute | solution.py:332

commit v3 on v2

v3 whole, which is shorter than its diff:
```python
import functools

import jax
import jax.numpy as jnp
from jax import lax
from jax.experimental import pallas as pl
from jax.experimental.pallas import tpu as pltpu
from jax.sharding import PartitionSpec as P


BLK = 32
LANES = 128
TILE = 256
SNAP_ROW = ("snap", "row")


def spread(mask, width):
    slots = mask.shape[1]
    slot = lax.broadcasted_iota(jnp.int32, (slots, width), 0)
    lane = lax.broadcasted_iota(jnp.int32, (slots, width), 1)
    chosen = (lane // BLK == slot).astype(jnp.bfloat16)
    return jnp.dot(
        mask.astype(jnp.bfloat16), chosen, preferred_element_type=jnp.float32
    )


def placed(rows, start, width):
    height, length = rows.shape
    if start < 0:
        rows = rows[:, -start:]
        length += start
        start = 0
    if start + length > width:
        length = width - start
        rows = rows[:, :length]
    parts = []
    if start:
        parts.append(jnp.zeros((height, start), rows.dtype))
    parts.append(rows)
    if start + length < width:
        parts.append(jnp.zeros((height, width - start - length), rows.dtype))
    return jnp.concatenate(parts, 1) if len(parts) > 1 else rows


def eye_sum(ref, lane_start):
    row = lax.broadcasted_iota(jnp.int32, (LANES, LANES), 0)
    lane = lax.broadcasted_iota(jnp.int32, (LANES, LANES), 1)
    total = jnp.zeros((1, LANES), jnp.float32)
    for k in range(ref.shape[0] // LANES):
        part = ref[pl.ds(k * LANES, LANES), pl.ds(lane_start + k * LANES, LANES)]
        part = jnp.where(row == lane, part.astype(jnp.float32), 0.0)
        total += jnp.sum(part, axis=0, keepdims=True)
    return total


def own_valid(block_rows, first_slot, slots, half_band):
    row = lax.broadcasted_iota(jnp.int32, (block_rows, slots), 0)
    slot = lax.broadcasted_iota(jnp.int32, (block_rows, slots), 1)
    column = lax.axis_index("row") * block_rows + row + first_slot + slot - half_band
    return (column >= 0) & (column < lax.axis_size("row") * block_rows)


def slot_kernel(chosen):
    slot = lax.broadcasted_iota(jnp.int32, chosen.shape, 0)
    lane = lax.broadcasted_iota(jnp.int32, chosen.shape, 1)
    chosen[...] = (lane // BLK == slot).astype(jnp.bfloat16)


def mask_kernel(chosen, pattern, keep_filter, mask):
    block_rows, slots = pattern.shape
    half = mask.shape[1]
    valid = own_valid(block_rows, lax.axis_index("col") * slots, slots, slots)
    own = jnp.where(valid, pattern[...], 0).astype(jnp.bfloat16)
    wide = jnp.dot(own, chosen[...], preferred_element_type=jnp.float32)
    mask[pl.ds(0, block_rows), :] = wide.astype(jnp.bfloat16)
    slot = lax.broadcasted_iota(jnp.int32, keep_filter.shape, 1)
    on_diagonal = jnp.where(slot == slots, keep_filter[...], 0).astype(jnp.float32)
    on_diagonal = jnp.sum(on_diagonal, axis=1, keepdims=True)
    mask[pl.ds(block_rows, block_rows), :] = jnp.broadcast_to(
        on_diagonal, (block_rows, half)
    ).astype(jnp.bfloat16)


def keep_kernel(density, mask, kept):
    height = density.shape[0]
    block_rows = height // BLK
    for i in range(block_rows):
        rows = pl.ds(i * BLK, BLK)
        kept[rows, :] = density[rows, :] * mask[pl.ds(i, 1), :]
    kept[pl.ds(height, block_rows), :] = mask[pl.ds(block_rows, block_rows), :]


def small_call(kernel, shape, scratch, flops, *operands, dtype=jnp.float32):
    vmem = pl.BlockSpec(memory_space=pltpu.VMEM)
    return pl.pallas_call(
        kernel,
        out_shape=jax.ShapeDtypeStruct(shape, dtype),
        in_specs=[vmem] * len(operands),
        out_specs=vmem,
        scratch_shapes=scratch,
        compiler_params=pltpu.CompilerParams(vmem_limit_bytes=16 * 1024 * 1024),
        cost_estimate=pl.CostEstimate(flops=flops, bytes_accessed=10**6, transcendentals=0),
    )(*operands)


def keep(density, pattern, keep_filter):
    height, half = density.shape
    block_rows = pattern.shape[0]
    chosen = small_call(slot_kernel, (pattern.shape[1], half), (), 10**10, dtype=density.dtype)
    mask = small_call(
        mask_kernel, (2 * block_rows, half), (), 10**3, chosen, pattern, keep_filter,
        dtype=density.dtype,
    )
    return small_call(
        keep_kernel, (height + block_rows, half), (), 10**9, density, mask,
        dtype=density.dtype,
    )


def joined(left, right):
    parts = [part for part in (left, right) if part.shape[1]]
    return jnp.concatenate(parts, 1) if len(parts) > 1 else parts[0]


def weighted_diagonal(a, b, weight):
    total = jnp.zeros((1, TILE), jnp.float32)
    row = lax.broadcasted_iota(jnp.int32, (TILE, TILE), 0)
    lane = lax.broadcasted_iota(jnp.int32, (TILE, TILE), 1)
    for m in range(a.shape[0] // TILE):
        at = pl.ds(m * TILE, TILE)
        prod = jnp.dot(a[at, :], b[:, at], preferred_element_type=jnp.float32)
        diagonal = jnp.sum(jnp.where(row == lane, prod, 0.0), axis=0, keepdims=True)
        total += diagonal * weight[:, m * TILE : (m + 1) * TILE]
    return jnp.sum(total)


def diagonal_weight(values):
    block = lax.broadcasted_iota(jnp.int32, values.shape, 0)
    lane = lax.broadcasted_iota(jnp.int32, values.shape, 1) // BLK
    values = jnp.where(block == lane, values.astype(jnp.float32), 0.0)
    return jnp.sum(values, axis=0, keepdims=True)


def inner_kernel(own_a, own_b, out_ref, square):
    half = own_a.shape[1]
    height = square.shape[0]
    block_rows = height // BLK
    first = lax.axis_index("col") == 0
    for i in range(block_rows):
        rows = pl.ds(i * BLK, BLK)
        cut = half - i * BLK
        a, b = own_a[rows, :], own_b[rows, :]
        left, right = jnp.where(first, a, b), jnp.where(first, b, a)
        square[rows, :] = joined(left[:, cut:], right[:, :cut])
    weight = diagonal_weight(own_a[pl.ds(height, block_rows), :])
    kept = jnp.sum(eye_sum(square, 0))
    inner = weighted_diagonal(square, square, weight)
    lane = lax.broadcasted_iota(jnp.int32, out_ref.shape, 1)
    out_ref[...] = jnp.where(lane == 0, kept, jnp.where(lane == 1, inner, 0.0))


def across_kernel(own_a, near, inner, out_ref, x_ref, y_ref):
    half = own_a.shape[1]
    height = x_ref.shape[0]
    block_rows = height // BLK
    first = lax.axis_index("col") == 0
    for i in range(block_rows):
        rows = pl.ds(i * BLK, BLK)
        cut = half - i * BLK
        a, b = own_a[rows, :], near[rows, :]
        upper, lower = jnp.where(first, b, a), jnp.where(first, a, b)
        gap = jnp.zeros((BLK, cut), jnp.bfloat16)
        x_ref[rows, :] = joined(upper[:, cut:], gap)
        gap = jnp.zeros((BLK, half - cut), jnp.bfloat16)
        y_ref[rows, :] = joined(gap, lower[:, :cut])
    below = pl.ds(height, block_rows)
    a, b = own_a[below, :], near[below, :]
    across = weighted_diagonal(x_ref, y_ref, diagonal_weight(jnp.where(first, b, a)))
    across += weighted_diagonal(y_ref, x_ref, diagonal_weight(jnp.where(first, a, b)))
    lane = lax.broadcasted_iota(jnp.int32, out_ref.shape, 1)
    out_ref[...] = jnp.where(lane == 2, across, inner[0:1, :])


def total_kernel(order, sums, out_ref):
    values = sums[...]
    moved = pltpu.roll(values, values.shape[0] - 1, 0)
    lane = lax.broadcasted_iota(jnp.int32, values.shape, 1)
    moves = lane + 128 * lax.axis_index("col") == 2
    values = jnp.sum(jnp.where(moves, moved, values), axis=0, keepdims=True)
    after = pltpu.roll(values, LANES - 1, 1)
    lane = lax.broadcasted_iota(jnp.int32, values.shape, 1)
    out_ref[...] = (jnp.where(lane == 1, values + after, values) / order)[0, :2]


def total(sums, order):
    vmem = pl.BlockSpec(memory_space=pltpu.VMEM)
    return pl.pallas_call(
        functools.partial(total_kernel, order),
        out_shape=jax.ShapeDtypeStruct((2,), jnp.float32),
        in_specs=[vmem],
        out_specs=vmem,
        compiler_params=pltpu.CompilerParams(vmem_limit_bytes=8 * 1024 * 1024),
        name="total",
    )(sums)


def purify_kernel(
    filter_ref, own_a, own_b, near, near_b, far, far_b,
    out_ref, band, full, sq, fmask, cube, sems,
):
    height, half = out_ref.shape
    block_rows = height // BLK
    slots = 2 * half // BLK
    col = lax.axis_index("col")
    mine = pl.multiple_of(col * half, half)
    other = pl.multiple_of((1 - col) * half, half)
    inner = 2 * col
    places = (
        (own_a, 1, mine), (own_b, 1, other), (near, inner, other),
        (near_b, 2 - inner, mine), (far, inner, mine), (far_b, 2 - inner, other),
    )
    copies = []
    for k, (src, row, lane) in enumerate(places):
        start = pl.multiple_of(row * height, height)
        copy = pltpu.make_async_copy(
            src.at[pl.ds(0, height), :],
            band.at[pl.ds(start, height), pl.ds(lane, half)],
            sems.at[k],
        )
        copy.start()
        copies.append(copy)
    width = full.shape[1]
    valid = own_valid(block_rows, 0, slots, slots // 2)
    wide = spread(jnp.where(valid, filter_ref[...], 0), slots * BLK)
    for i in range(block_rows):
        fmask[pl.ds(i, 1), :] = placed(wide[i : i + 1], i * BLK, width)

    def skew(row):
        for r in range(row * block_rows, (row + 1) * block_rows):
            rows = band[pl.ds(r * BLK, BLK), :]
            full[pl.ds(r * BLK, BLK), :] = placed(rows, (r - block_rows) * BLK, width)

    copies[0].wait()
    copies[1].wait()
    skew(1)
    for copy in copies[2:]:
        copy.wait()
    skew(0)
    skew(2)
    tiles = height // TILE
    span = (block_rows * 2 + TILE // BLK - 1) * BLK
    span = -(-span // TILE)
    reach = height // TILE
    per_tile = TILE // BLK
    sq[...] = jnp.zeros_like(sq)
    for m in range(tiles):
        for b in range(m, m + span):
            first = max(b - reach, m)
            last = min(b + reach, m + span - 1)
            k0, klen = first * TILE, (last - first + 1) * TILE
            prod = jnp.dot(
                full[pl.ds(height + m * TILE, TILE), pl.ds(k0, klen)],
                full[pl.ds(k0, klen), pl.ds(b * TILE, TILE)],
                preferred_element_type=jnp.float32,
            )
            for i in range(per_tile):
                row = m * per_tile + i
                keep = fmask[pl.ds(row, 1), pl.ds(b * TILE, TILE)]
                sq[pl.ds(row * BLK, BLK), pl.ds(b * TILE, TILE)] = (
                    prod[i * BLK : (i + 1) * BLK] * keep
                ).astype(jnp.bfloat16)
    out_span = half // TILE + 1
    for m in range(tiles):
        lanes = pl.multiple_of(m * TILE + col * half, TILE)
        cube[...] = jnp.dot(
            sq[pl.ds(m * TILE, TILE), pl.ds(m * TILE, span * TILE)],
            full[pl.ds(m * TILE, span * TILE), pl.ds(lanes, out_span * TILE)],
            preferred_element_type=jnp.float32,
        )
        for i in range(per_tile):
            row = m * per_tile + i
            base = i * BLK // LANES * LANES
            shift = i * BLK - base
            size = half + (LANES if shift else 0)
            at = pl.ds(pl.multiple_of(m * TILE + base + col * half, LANES), size)
            kept = sq[pl.ds(row * BLK, BLK), at].astype(jnp.float32)
            keep = fmask[pl.ds(row, 1), at]
            part = cube[pl.ds(i * BLK, BLK), pl.ds(base, size)]
            result = (3.0 * kept - 2.0 * (part * keep)).astype(jnp.bfloat16)
            out_ref[pl.ds(row * BLK, BLK), :] = result[:, shift : shift + half]


def purify(keep_filter, height, *pieces):
    half = pieces[0].shape[1]
    width = 3 * height
    block_rows = height // BLK
    anywhere = pl.BlockSpec(memory_space=pl.ANY)
    vmem = pl.BlockSpec(memory_space=pltpu.VMEM)
    return pl.pallas_call(
        purify_kernel,
        out_shape=jax.ShapeDtypeStruct((height, half), jnp.bfloat16),
        in_specs=[vmem] + [anywhere] * 6,
        out_specs=vmem,
        scratch_shapes=[
            pltpu.VMEM((width, 2 * half), jnp.bfloat16),
            pltpu.VMEM((width, width), jnp.bfloat16),
            pltpu.VMEM((height, width), jnp.bfloat16),
            pltpu.VMEM((block_rows, width), jnp.float32),
            pltpu.VMEM((TILE, half + TILE), jnp.float32),
            pltpu.SemaphoreType.DMA((6,)),
        ],
        compiler_params=pltpu.CompilerParams(vmem_limit_bytes=48 * 1024 * 1024),
        cost_estimate=pl.CostEstimate(flops=3 * 10**9, bytes_accessed=4 * 10**6, transcendentals=0),
        name="purify",
    )(keep_filter, *pieces)


def per_device(density, pattern, filter_mask):
    size = lax.axis_size("row")
    kept = keep(density, pattern, filter_mask)

    def device(row, col):
        return 2 * row + col

    def exchanged(value):
        pairs = [(device(i, 1), device(i + 1, 0)) for i in range(size - 1)]
        return lax.ppermute(value, ("row", "col"), pairs + [(b, a) for a, b in pairs])

    def shifted(value):
        pairs = [(device(i, 0), device(i + 1, 0)) for i in range(size - 1)]
        pairs += [(device(i + 1, 1), device(i, 1)) for i in range(size - 1)]
        return lax.ppermute(value, ("row", "col"), pairs)

    def swapped(value):
        return lax.ppermute(value, "col", [(0, 1), (1, 0)])

    half = density.shape[1]
    square = pltpu.VMEM((half, half), jnp.bfloat16)
    near = exchanged(kept)
    own_b = swapped(kept)
    sums = small_call(inner_kernel, (8, LANES), [square], 10**9, kept, own_b)
    far = shifted(kept)
    sums = small_call(across_kernel, (size, LANES), [square] * 2, 10**9, kept, near, sums)
    sums = sums.reshape(size, 1, LANES)
    sums = lax.all_to_all(sums, "row", split_axis=0, concat_axis=0, tiled=True)
    sums = sums.reshape(size, LANES)
    near_b = swapped(near)
    far_b = swapped(far)
    purified = purify(
        filter_mask, density.shape[0], kept, own_b, near, near_b, far, far_b
    )
    return purified, total(sums, size * density.shape[0])


def solution(mesh):
    placed_as = (P(SNAP_ROW, "col"), P(SNAP_ROW, "col"), P(SNAP_ROW, None))
    return jax.shard_map(
        per_device,
        mesh=mesh,
        in_specs=placed_as,
        out_specs=(P(SNAP_ROW, "col"), P("snap")),
        check_vma=False,
    )
```

time: 100 us -> 98 us (0.980)
  blocking collectives: 32.4 us -> 35.5 us
  starting transfers between devices: 56 us -> 53.4 us
  Pallas kernels: 8.86 us -> 6.78 us
    all_to_all x1, blocking collectives: 32.4 us -> 35.5 us  [per_device(): sums = lax.all_to_all(sums, 'row', split_axis=0, concat_axis=0, tiled=True)]
    ppermute x3, starting transfers between devices: 48.3 us -> 45.3 us  [swapped(): return lax.ppermute(value, 'col', [(0, 1), (1, 0)])]
    pallas_call x3 -> x6, Pallas kernels: 3.65 us -> 2.04 us  [the longest x5 1.43 us: small_call(): pl.pallas_call(kernel, out_shape=jax.ShapeDtypeStruct(shape, dtype), in_s...]
    ppermute x0 -> x1, starting transfers between devices: none -> 1.31 us  [shifted(): return lax.ppermute(value, ('row', 'col'), pairs)]
    ppermute x2 -> x1, starting transfers between devices: 7.67 us -> 6.85 us  [exchanged(): lax.ppermute(value, ('row', 'col'), pairs + [(b, a) for a, b in pairs])]
  transfers between devices with their start and end apart: 5 -> 5, of which waited for: 0 -> 0; matrix products, arithmetic and copies ran while one was open for 0% -> 0% of each run, Pallas kernels for 3% -> 2%
where the time goes in v3:
time: 98 us; the launch traced here: 97.3 us
  starting transfers between devices  53.4 us (54%)
  blocking collectives  35.5 us (36%)
  Pallas kernels  6.78 us (7%)
    ppermute x3, starting transfers between devices, swapped(): return lax.ppermute(value, 'col', [(0, 1), (1, 0)])  45.3 us
    all_to_all x1, blocking collectives, per_device(): sums = lax.all_to_all(sums, 'row', split_axis=0, concat_axis=0, tiled=True)  35.5 us
    ppermute x1, starting transfers between devices, exchanged(): lax.ppermute(value, ('row', 'col'), pairs + [(b, a) for a, b in pairs])  6.85 us
    pallas_call x1, Pallas kernels, purify(): pl.pallas_call(purify_kernel, out_shape=jax.ShapeDtypeStruct((height, hal...  4.74 us
  transfers between devices with their start and end apart: 5, of which 0 were waited for; matrix products, arithmetic and copies ran while one was open for 0% of the time, Pallas kernels for 2%

profile of v3, /device:TPU:65, one launch (start us, length us, event | category | flops | bytes accessed | tf_op | source)
XLA Modules:
  0.0 97.3 jit_solution(3325146320472727797)
XLA Ops:
  0.6 0.0 copy-start.1
  0.6 0.0 copy-start
  0.6 0.0 copy-start.2
  0.7 0.7 copy-done.1
  1.3 0.0 copy-done
  1.3 0.1 shard_map.51.mask
  1.5 0.2 copy-done.2
  1.7 0.1 shard_map.52.own_a
  1.8 1.3 %collective-permute-start.3 = (bf16[528,512]{1,0:T(8,128)(2,1)S(1)}, bf16[528,512]{1,0:T(8,128)(2,1)S(1)}, u32[]{:S(2)}, u32[]{:S(2)}) collective-permute-start(bf16[528,512]{1,0:T(8,128)(2,1)S(1)} %shard_map.52.own_a), channel_id=1, source_target_pairs={{0,2},{2,4},{4,6},{6,8},{8,10},{10,12},{12,14},{14,16},{16,18},{18... | collective-permute-start | bytes 1622024 | tf_op jit(solution)/shard_map/ppermute | solution.py:332
  3.1 6.9 %collective-permute-start.1 = (bf16[528,512]{1,0:T(8,128)(2,1)S(1)}, bf16[528,512]{1,0:T(8,128)(2,1)S(1)}, u32[]{:S(2)}, u32[]{:S(2)}) collective-permute-start(bf16[528,512]{1,0:T(8,128)(2,1)S(1)} %shard_map.52.own_a), channel_id=1, source_target_pairs={{1,2},{3,4},{5,6},{7,8},{9,10},{11,12},{13,14},{15,16},{17,18},{19... | collective-permute-start | bytes 1622024 | tf_op jit(solution)/shard_map/ppermute | solution.py:327
  9.9 37.2 %collective-permute-start = (bf16[528,512]{1,0:T(8,128)(2,1)S(1)}, bf16[528,512]{1,0:T(8,128)(2,1)S(1)}, u32[]{:S(2)}, u32[]{:S(2)}) collective-permute-start(bf16[528,512]{1,0:T(8,128)(2,1)S(1)} %shard_map.52.own_a), channel_id=1, source_target_pairs={{0,1},{1,0},{2,3},{3,2},{4,5},{5,4},{6,7},{7,6},{8,9},{9,8},{10,11... | collective-permute-start | bytes 1622024 | tf_op jit(solution)/shard_map/ppermute | solution.py:335
  47.2 0.0 collective-permute-done.3.far
  47.2 6.1 %collective-permute-start.4 = (bf16[528,512]{1,0:T(8,128)(2,1)S(1)}, bf16[528,512]{1,0:T(8,128)(2,1)S(1)}, u32[]{:S(2)}, u32[]{:S(2)}) collective-permute-start(bf16[528,512]{1,0:T(8,128)(2,1)S(1)} %collective-permute-done.3.far), channel_id=1, source_target_pairs={{0,1},{1,0},{2,3},{3,2},{4,5},{5,4},{6,7},{7,6},{8,9},{9,8},{10,11... | collective-permute-start | bytes 1622024 | tf_op jit(solution)/shard_map/ppermute | solution.py:335
  53.3 0.0 collective-permute-done.1.near
  53.3 2.0 %collective-permute-start.2 = (bf16[528,512]{1,0:T(8,128)(2,1)S(1)}, bf16[528,512]{1,0:T(8,128)(2,1)S(1)}, u32[]{:S(2)}, u32[]{:S(2)}) collective-permute-start(bf16[528,512]{1,0:T(8,128)(2,1)S(1)} %collective-permute-done.1.near), channel_id=1, source_target_pairs={{0,1},{1,0},{2,3},{3,2},{4,5},{5,4},{6,7},{7,6},{8,9},{9,8},{10,11... | collective-permute-start | bytes 1622024 | tf_op jit(solution)/shard_map/ppermute | solution.py:335
  55.3 0.0 collective-permute-done.own_b
  55.3 0.6 shard_map.53.inner
  55.8 0.7 shard_map.54
  56.5 35.5 %all_to_all.5 = f32[128,1,128]{2,1,0:T(1,128)S(1)} all-to-all(f32[128,1,128]{2,1,0:T(1,128)S(1)} %bitcast.5), channel_id=1, replica_groups=mesh['snap'=2,'row'=128,'col'=2] {'row'}, dimensions={0} | all-to-all | bytes 131072 | tf_op jit(solution)/shard_map/all_to_all | solution.py:345
  92.0 0.6 total.1
  92.6 0.0 collective-permute-done.4.far_b
  92.6 0.0 collective-permute-done.2.near_b
  92.6 4.7 %purify.1 = bf16[512,512]{1,0:T(8,128)(2,1)} custom-call(s32[16,32]{1,0:T(8,128)S(1)} %copy-done.1, bf16[528,512]{1,0:T(8,128)(2,1)S(1)} %shard_map.52.own_a, bf16[528,512]{1,0:T(8,128)(2,1)S(1)} %collective-permute-done.own_b, bf16[528,512]{1,0:T(8,128)(2,1)S(1)} %collective-permute-done.1.near, bf16[528,512]{1,0:T(8,128)(2,1)S(1)} %collective-permute-done.2.near_b, ...), custom_call_target="tpu_custom_call" | custom-call | flops 3000000000 | bytes 4000000 | tf_op jit(solution)/shard_map/purify/pallas_call | solution.py:299
  (1 shorter events, 0.0 us)
Async XLA Ops:
  0.6 0.7 copy-start.1
  0.6 0.7 copy-start
  0.6 1.1 %copy-start.2 = (bf16[512,512]{1,0:T(8,128)(2,1)S(1)}, bf16[512,512]{1,0:T(8,128)(2,1)}, u32[]{:S(2)}) copy-start(bf16[512,512]{1,0:T(8,128)(2,1)} %density.1) | copy-start | bytes 1572868
  1.8 45.4 %collective-permute-start.3 = (bf16[528,512]{1,0:T(8,128)(2,1)S(1)}, bf16[528,512]{1,0:T(8,128)(2,1)S(1)}, u32[]{:S(2)}, u32[]{:S(2)}) collective-permute-start(bf16[528,512]{1,0:T(8,128)(2,1)S(1)} %shard_map.52.own_a), channel_id=1, source_target_pairs={{0,2},{2,4},{4,6},{6,8},{8,10},{10,12},{12,14},{14,16},{16,18},{18... | collective-permute-start | bytes 1622024 | tf_op jit(solution)/shard_map/ppermute | solution.py:332
  3.1 50.2 %collective-permute-start.1 = (bf16[528,512]{1,0:T(8,128)(2,1)S(1)}, bf16[528,512]{1,0:T(8,128)(2,1)S(1)}, u32[]{:S(2)}, u32[]{:S(2)}) collective-permute-start(bf16[528,512]{1,0:T(8,128)(2,1)S(1)} %shard_map.52.own_a), channel_id=1, source_target_pairs={{1,2},{3,4},{5,6},{7,8},{9,10},{11,12},{13,14},{15,16},{17,18},{19... | collective-permute-start | bytes 1622024 | tf_op jit(solution)/shard_map/ppermute | solution.py:327
  9.9 45.3 %collective-permute-start = (bf16[528,512]{1,0:T(8,128)(2,1)S(1)}, bf16[528,512]{1,0:T(8,128)(2,1)S(1)}, u32[]{:S(2)}, u32[]{:S(2)}) collective-permute-start(bf16[528,512]{1,0:T(8,128)(2,1)S(1)} %shard_map.52.own_a), channel_id=1, source_target_pairs={{0,1},{1,0},{2,3},{3,2},{4,5},{5,4},{6,7},{7,6},{8,9},{9,8},{10,11... | collective-permute-start | bytes 1622024 | tf_op jit(solution)/shard_map/ppermute | solution.py:335
  47.2 45.4 %collective-permute-start.4 = (bf16[528,512]{1,0:T(8,128)(2,1)S(1)}, bf16[528,512]{1,0:T(8,128)(2,1)S(1)}, u32[]{:S(2)}, u32[]{:S(2)}) collective-permute-start(bf16[528,512]{1,0:T(8,128)(2,1)S(1)} %collective-permute-done.3.far), channel_id=1, source_target_pairs={{0,1},{1,0},{2,3},{3,2},{4,5},{5,4},{6,7},{7,6},{8,9},{9,8},{10,11... | collective-permute-start | bytes 1622024 | tf_op jit(solution)/shard_map/ppermute | solution.py:335
  53.3 39.3 %collective-permute-start.2 = (bf16[528,512]{1,0:T(8,128)(2,1)S(1)}, bf16[528,512]{1,0:T(8,128)(2,1)S(1)}, u32[]{:S(2)}, u32[]{:S(2)}) collective-permute-start(bf16[528,512]{1,0:T(8,128)(2,1)S(1)} %collective-permute-done.1.near), channel_id=1, source_target_pairs={{0,1},{1,0},{2,3},{3,2},{4,5},{5,4},{6,7},{7,6},{8,9},{9,8},{10,11... | collective-permute-start | bytes 1622024 | tf_op jit(solution)/shard_map/ppermute | solution.py:335
